TPU v7x, 32 devices: a whole 2x2x4 slice. The times are simulated.
32 devices in a mesh: occ: 8 (over z, x), rep: 4 (over y, core).
Axes of the slice: x: 2, y: 2, z: 4, core: 2. Of those that a mesh axis runs over, the one named last changes fastest.
Arguments:
- coeffs: bfloat16 [128, 12, 64, 128], P(('occ', 'rep')), may hold values from -1 to 1
- amplitudes: bfloat16 [128, 4096], P(('occ', 'rep')), may hold values from -6 to 6
- denominators: float32 [128, 64], P(('occ', 'rep')), may hold values from 0.25 to 2
- pno_count: int32 [128], P(('occ', 'rep')), may hold values from 24 to 64
- domains: int32 [128, 12], replicated, may hold values from 0 to 31, as said below
- far_owner: int32 [128, 2], P(('occ', 'rep')), may hold values from 0 to 7, all different within a row; in each aligned block of 4 rows (0 to 3, 4 to 7, ...) at most 2 rows name the same one
- far_pair: int32 [128, 2], P(('occ', 'rep')), may hold values from 0 to 3
- near_pair: int32 [128, 40], P(('occ', 'rep')), may hold values from 0 to 15
Outputs:
- residual: float32 [128, 4096], P(('occ', 'rep'))
Inputs may be any that keep to these rules, and one draw needn't show every extreme that they name: `domains`: each row names 12 different blocks. `far_owner`: the 2 entries of a row differ; among the rows of one device no occupied block is named more than 2 times, and that bound is reached.
All inputs are finite; a program needn't handle non-finite values.
Results may differ from a plain program's by a relative error of at most 0.0003.
Values may be sent and summed in bfloat16 or wider, within the bound.
No kernel may reach another device: no remote copies, remote signals or barrier semaphores. Data moves between devices by JAX's collectives and lax.ppermute only.
A program may use at most 128 MiB of HBM per device.

v0:
```python
import jax
import jax.numpy as jnp
from jax import lax
from jax.sharding import PartitionSpec as P

NPNO = 64
KN = 2


def intersection(left_coeff, left_dom, right_coeff, right_dom):
    matches = (left_dom[:, None] == right_dom[None, :]).astype(jnp.bfloat16)
    flat = right_coeff.reshape(right_coeff.shape[0], -1)
    aligned = (
        jnp.dot(matches, flat, preferred_element_type=jnp.float32)
        .astype(jnp.bfloat16)
        .reshape(right_coeff.shape)
    )
    per_block = jnp.einsum("arc,asc->ars", left_coeff, aligned, preferred_element_type=jnp.float32)
    return jnp.sum(per_block, axis=0)


def square_amps(amplitude):
    return amplitude.reshape(amplitude.shape[0], NPNO, NPNO).astype(jnp.float32)


def carry_each(intersections, amplitude):
    return jnp.einsum(
        "kab,kbc,kdc->kad",
        intersections,
        square_amps(amplitude),
        intersections,
        precision=lax.Precision.HIGHEST,
    )


def carry_back(intersections, amplitude):
    return jnp.einsum(
        "kba,kbc,kcd->kad",
        intersections,
        square_amps(amplitude),
        intersections,
        precision=lax.Precision.HIGHEST,
    )


def on_device(coeffs, amplitudes, denominators, pno_count, domains, far_owner, far_pair, near_pair):
    pair_count = coeffs.shape[0]
    occ_count = lax.axis_size("occ")
    rep_count = lax.axis_size("rep")
    capacity = max(2, 2 * pair_count * KN // occ_count)
    occ_index = lax.axis_index("occ")
    rep_index = lax.axis_index("rep")
    device = occ_index * rep_count + rep_index
    live_rows = jnp.arange(NPNO, dtype=jnp.int32)[None, :] < pno_count[:, None]
    live_both = live_rows[:, :, None] & live_rows[:, None, :]
    coeff_masked = jnp.where(live_rows[:, None, :, None], coeffs, jnp.zeros((), jnp.bfloat16))
    amp_masked = jnp.where(
        live_both.reshape(pair_count, -1), amplitudes, jnp.zeros((), jnp.bfloat16)
    )
    home_dom = lax.dynamic_slice_in_dim(domains, device * pair_count, pair_count, 0)
    group_coeff, group_amp = (
        lax.all_gather(coeff_masked, "rep", axis=0, tiled=True),
        lax.all_gather(amp_masked, "rep", axis=0, tiled=True),
    )
    group_dom = lax.dynamic_slice_in_dim(
        domains, occ_index * rep_count * pair_count, rep_count * pair_count, 0
    )

    def near_term(operands):
        left_coeff, left_dom, chosen = operands
        intersections = jax.vmap(intersection, in_axes=(None, None, 0, 0))(
            left_coeff, left_dom, group_coeff[chosen], group_dom[chosen]
        )
        return jnp.sum(carry_each(intersections, group_amp[chosen]), axis=0)

    near_gain = lax.map(near_term, (coeff_masked, home_dom, near_pair))
    owner_flat = far_owner.reshape(-1)
    pair_flat = far_pair.reshape(-1)
    source_pair = jnp.repeat(jnp.arange(pair_count, dtype=jnp.int32), KN)
    owner_hot = (owner_flat[:, None] == jnp.arange(occ_count, dtype=jnp.int32)[None, :]).astype(
        jnp.int32
    )
    earlier = jnp.cumsum(owner_hot, axis=0) - owner_hot
    slot_index = jnp.sum(earlier * owner_hot, axis=1)
    slot_hot = (slot_index[:, None] == jnp.arange(capacity, dtype=jnp.int32)[None, :]).astype(
        jnp.int32
    )
    position = owner_flat * capacity + slot_index
    slot_total = occ_count * capacity
    block_shape = coeffs.shape[1:]

    def slot_table(values):
        return jnp.einsum("rd,rs->ds", owner_hot * (values + 1)[:, None], slot_hot)

    targets = slot_table(pair_flat)
    sources = slot_table(source_pair)
    recv_target, recv_source = (
        lax.all_to_all(targets, "occ", split_axis=0, concat_axis=0, tiled=True),
        lax.all_to_all(sources, "occ", split_axis=0, concat_axis=0, tiled=True),
    )
    filled = targets > 0
    picked = jnp.maximum(sources - 1, 0)
    send_coeff = jnp.where(
        filled[:, :, None, None, None], coeff_masked[picked], jnp.zeros((), jnp.bfloat16)
    )
    send_amps = jnp.where(filled[:, :, None], amp_masked[picked], jnp.zeros((), jnp.bfloat16))
    recv_coeff, recv_amps = (
        lax.all_to_all(send_coeff, "occ", split_axis=0, concat_axis=0, tiled=True),
        lax.all_to_all(send_amps, "occ", split_axis=0, concat_axis=0, tiled=True),
    )
    target_flat = recv_target.reshape(-1)
    local_target = jnp.maximum(target_flat - 1, 0)
    sender_block = jnp.arange(occ_count, dtype=jnp.int32)[:, None]
    sender_ids = (
        (sender_block * rep_count + rep_index) * pair_count + jnp.maximum(recv_source - 1, 0)
    ).reshape(-1)
    intersections = jax.vmap(intersection)(
        recv_coeff.reshape((slot_total,) + block_shape),
        domains[sender_ids],
        coeff_masked[local_target],
        home_dom[local_target],
    )
    slot_gain = carry_each(intersections, amp_masked[local_target]).reshape(occ_count, capacity, -1)
    back_terms = carry_back(intersections, recv_amps.reshape(slot_total, -1)).reshape(
        slot_total, -1
    )
    replies = lax.all_to_all(slot_gain, "occ", split_axis=0, concat_axis=0, tiled=True)
    far_gain = (
        replies.reshape(slot_total, -1)[position].reshape(pair_count, KN, NPNO, NPNO).sum(axis=1)
    )
    receivers = jnp.where(target_flat > 0, target_flat - 1, -1)
    owner_table = (jnp.arange(pair_count, dtype=jnp.int32)[:, None] == receivers[None, :]).astype(
        jnp.float32
    )
    back_sum = jnp.dot(owner_table, back_terms, precision=lax.Precision.HIGHEST)
    denominator_sum = denominators[:, :, None] + denominators[:, None, :]
    residual = (
        denominator_sum * square_amps(amp_masked)
        + near_gain
        + far_gain
        + back_sum.reshape(pair_count, NPNO, NPNO)
    )
    residual = jnp.where(live_both, residual, jnp.zeros((), jnp.float32))
    return residual.reshape(pair_count, NPNO * NPNO)


def solution(mesh):
    in_specs = (
        P(("occ", "rep"), None, None, None),
        P(("occ", "rep"), None),
        P(("occ", "rep"), None),
        P(("occ", "rep")),
        P(),
        P(("occ", "rep"), None),
        P(("occ", "rep"), None),
        P(("occ", "rep"), None),
    )
    out_specs = P(("occ", "rep"), None)
    return jax.shard_map(
        on_device, mesh=mesh, in_specs=in_specs, out_specs=out_specs, check_vma=False
    )
```

profile of v0, /device:TPU:8, one launch (start us, length us, event | category | flops | bytes accessed | tf_op | source)
XLA Modules:
  0.0 345.6 jit_solution(10821142017348831139)
XLA Ops:
  8.8 6.3 %all-to-all-start.2 = ((s32[8,1,2]{2,1,0:T(1,128)}), s32[8,1,2]{2,1,0:T(1,128)S(1)}, u32[]{:S(2)}, u32[]{:S(2)}) async-start(s32[8,1,2]{2,1,0:T(1,128)} %copy.144), calls=%async_computation.2 | async-start | bytes 8192 | tf_op jit(solution)/shard_map/all_to_all | solution.py:99
  56.3 6.1 %reshape.377 = bf16[16,12,8192]{2,1,0:T(8,128)(2,1)} reshape(bf16[16,12,64,128]{3,2,1,0:T(8,128)(2,1)} %gather_fusion.7) | data formatting | bytes 6291456 | tf_op jit(solution)/shard_map/vmap()/reshape | solution.py:12
  68.5 6.2 %reshape.378 = bf16[16,12,64,128]{3,2,1,0:T(8,128)(2,1)} reshape(bf16[16,12,8192]{2,1,0:T(8,128)(2,1)} %convolution_convert_fusion.1) | data formatting | bytes 6291456 | tf_op jit(solution)/shard_map/vmap()/reshape | solution.py:16
  82.0 236.0 %while.11 = (s32[]{:T(128)}, f32[4,64,64]{2,0,1:T(4,128)}, s32[4,40]{1,0:T(4,128)}, bf16[16,4096]{1,0:T(8,128)(2,1)S(1)}, bf16[4,12,64,128]{3,2,1,0:T(8,128)(2,1...) while((s32[]{:T(128)}, f32[4,64,64]{2,0,1:T(4,128)}, ...), condition=%wide.region_1.2_spmd.clone, body=%wide.region_0.1_spmd.sunk.clone | while | flops 853285632 | bytes 75950904 | solution.py:76
  82.7 7.8 %gather_fusion.1 = bf16[40,12,64,128]{3,2,1,0:T(8,128)(2,1)} fusion(bf16[16,12,64,128]{3,2,1,0:T(8,128)(2,1)} %get-tuple-element.202, s32[1024]{0:T(1024)S(1)} %pad_clamp_fusion.7), kind=kCustom, calls=%fused_computation.2.clone.1.clone | custom fusion | bytes 15728800 | tf_op jit(solution)/shard_map/while/body/eval_jaxpr/gather | solution.py:72
  90.4 13.3 %reshape.421 = bf16[40,12,8192]{2,1,0:T(8,128)(2,1)} reshape(bf16[40,12,64,128]{3,2,1,0:T(8,128)(2,1)} %gather_fusion.1) | data formatting | bytes 15728640 | tf_op jit(solution)/shard_map/while/body/eval_jaxpr/vmap()/reshape | solution.py:12
  104.3 10.7 %convolution_convert_fusion.4 = bf16[40,12,8192]{2,1,0:T(8,128)(2,1)} fusion(bf16[40,12,8192]{2,1,0:T(8,128)(2,1)} %reshape.421, s32[40,12]{1,0:T(8,128)S(1)} %gather_fusion.2, s32[12]{0:T(128)S(1)} %fusion.92), kind=kOutput, calls=%fused_computation.10.clone.1.clone | convolution fusion | flops 98309760 | bytes 15730608 | tf_op jit(solution)/shard_map/while/body/eval_jaxpr/vmap()/dot_general | solution.py:14
  115.0 13.6 %reshape.422 = bf16[40,12,64,128]{3,2,1,0:T(8,128)(2,1)} reshape(bf16[40,12,8192]{2,1,0:T(8,128)(2,1)} %convolution_convert_fusion.4) | data formatting | bytes 15728640 | tf_op jit(solution)/shard_map/while/body/eval_jaxpr/vmap()/reshape | solution.py:16
  128.7 7.0 %convolution_bitcast_fusion.4 = f32[40,64,64]{2,1,0:T(8,128)S(1)} fusion(bf16[40,12,64,128]{3,2,1,0:T(8,128)(2,1)} %reshape.422, bf16[4,12,64,128]{3,2,1,0:T(8,128)(2,1)S(1)} %get-tuple-element.199, s32[]{:T(128)} %get-tuple-element.187), kind=kOutput, calls=%fused_computation.11.clone.1.clone | convolution fusion | flops 503316480 | bytes 8716292 | tf_op jit(solution)/shard_map/while/body/eval_jaxpr/vmap(arc,asc->ars)/dot_general | solution.py:18
  141.7 7.8 %gather_fusion.1 = bf16[40,12,64,128]{3,2,1,0:T(8,128)(2,1)} fusion(bf16[16,12,64,128]{3,2,1,0:T(8,128)(2,1)} %get-tuple-element.202, s32[1024]{0:T(1024)S(1)} %pad_clamp_fusion.7), kind=kCustom, calls=%fused_computation.2.clone.1.clone | custom fusion | bytes 15728800 | tf_op jit(solution)/shard_map/while/body/eval_jaxpr/gather | solution.py:72
  149.5 13.3 %reshape.421 = bf16[40,12,8192]{2,1,0:T(8,128)(2,1)} reshape(bf16[40,12,64,128]{3,2,1,0:T(8,128)(2,1)} %gather_fusion.1) | data formatting | bytes 15728640 | tf_op jit(solution)/shard_map/while/body/eval_jaxpr/vmap()/reshape | solution.py:12
  163.3 10.7 %convolution_convert_fusion.4 = bf16[40,12,8192]{2,1,0:T(8,128)(2,1)} fusion(bf16[40,12,8192]{2,1,0:T(8,128)(2,1)} %reshape.421, s32[40,12]{1,0:T(8,128)S(1)} %gather_fusion.2, s32[12]{0:T(128)S(1)} %fusion.92), kind=kOutput, calls=%fused_computation.10.clone.1.clone | convolution fusion | flops 98309760 | bytes 15730608 | tf_op jit(solution)/shard_map/while/body/eval_jaxpr/vmap()/dot_general | solution.py:14
  174.1 13.6 %reshape.422 = bf16[40,12,64,128]{3,2,1,0:T(8,128)(2,1)} reshape(bf16[40,12,8192]{2,1,0:T(8,128)(2,1)} %convolution_convert_fusion.4) | data formatting | bytes 15728640 | tf_op jit(solution)/shard_map/while/body/eval_jaxpr/vmap()/reshape | solution.py:16
  187.7 7.0 %convolution_bitcast_fusion.4 = f32[40,64,64]{2,1,0:T(8,128)S(1)} fusion(bf16[40,12,64,128]{3,2,1,0:T(8,128)(2,1)} %reshape.422, bf16[4,12,64,128]{3,2,1,0:T(8,128)(2,1)S(1)} %get-tuple-element.199, s32[]{:T(128)} %get-tuple-element.187), kind=kOutput, calls=%fused_computation.11.clone.1.clone | convolution fusion | flops 503316480 | bytes 8716292 | tf_op jit(solution)/shard_map/while/body/eval_jaxpr/vmap(arc,asc->ars)/dot_general | solution.py:18
  200.7 7.8 %gather_fusion.1 = bf16[40,12,64,128]{3,2,1,0:T(8,128)(2,1)} fusion(bf16[16,12,64,128]{3,2,1,0:T(8,128)(2,1)} %get-tuple-element.202, s32[1024]{0:T(1024)S(1)} %pad_clamp_fusion.7), kind=kCustom, calls=%fused_computation.2.clone.1.clone | custom fusion | bytes 15728800 | tf_op jit(solution)/shard_map/while/body/eval_jaxpr/gather | solution.py:72
  208.5 13.3 %reshape.421 = bf16[40,12,8192]{2,1,0:T(8,128)(2,1)} reshape(bf16[40,12,64,128]{3,2,1,0:T(8,128)(2,1)} %gather_fusion.1) | data formatting | bytes 15728640 | tf_op jit(solution)/shard_map/while/body/eval_jaxpr/vmap()/reshape | solution.py:12
  222.3 10.7 %convolution_convert_fusion.4 = bf16[40,12,8192]{2,1,0:T(8,128)(2,1)} fusion(bf16[40,12,8192]{2,1,0:T(8,128)(2,1)} %reshape.421, s32[40,12]{1,0:T(8,128)S(1)} %gather_fusion.2, s32[12]{0:T(128)S(1)} %fusion.92), kind=kOutput, calls=%fused_computation.10.clone.1.clone | convolution fusion | flops 98309760 | bytes 15730608 | tf_op jit(solution)/shard_map/while/body/eval_jaxpr/vmap()/dot_general | solution.py:14
  233.1 13.6 %reshape.422 = bf16[40,12,64,128]{3,2,1,0:T(8,128)(2,1)} reshape(bf16[40,12,8192]{2,1,0:T(8,128)(2,1)} %convolution_convert_fusion.4) | data formatting | bytes 15728640 | tf_op jit(solution)/shard_map/while/body/eval_jaxpr/vmap()/reshape | solution.py:16
  246.7 7.0 %convolution_bitcast_fusion.4 = f32[40,64,64]{2,1,0:T(8,128)S(1)} fusion(bf16[40,12,64,128]{3,2,1,0:T(8,128)(2,1)} %reshape.422, bf16[4,12,64,128]{3,2,1,0:T(8,128)(2,1)S(1)} %get-tuple-element.199, s32[]{:T(128)} %get-tuple-element.187), kind=kOutput, calls=%fused_computation.11.clone.1.clone | convolution fusion | flops 503316480 | bytes 8716292 | tf_op jit(solution)/shard_map/while/body/eval_jaxpr/vmap(arc,asc->ars)/dot_general | solution.py:18
  259.7 7.8 %gather_fusion.1 = bf16[40,12,64,128]{3,2,1,0:T(8,128)(2,1)} fusion(bf16[16,12,64,128]{3,2,1,0:T(8,128)(2,1)} %get-tuple-element.202, s32[1024]{0:T(1024)S(1)} %pad_clamp_fusion.7), kind=kCustom, calls=%fused_computation.2.clone.1.clone | custom fusion | bytes 15728800 | tf_op jit(solution)/shard_map/while/body/eval_jaxpr/gather | solution.py:72
  267.5 13.3 %reshape.421 = bf16[40,12,8192]{2,1,0:T(8,128)(2,1)} reshape(bf16[40,12,64,128]{3,2,1,0:T(8,128)(2,1)} %gather_fusion.1) | data formatting | bytes 15728640 | tf_op jit(solution)/shard_map/while/body/eval_jaxpr/vmap()/reshape | solution.py:12
  281.3 10.7 %convolution_convert_fusion.4 = bf16[40,12,8192]{2,1,0:T(8,128)(2,1)} fusion(bf16[40,12,8192]{2,1,0:T(8,128)(2,1)} %reshape.421, s32[40,12]{1,0:T(8,128)S(1)} %gather_fusion.2, s32[12]{0:T(128)S(1)} %fusion.92), kind=kOutput, calls=%fused_computation.10.clone.1.clone | convolution fusion | flops 98309760 | bytes 15730608 | tf_op jit(solution)/shard_map/while/body/eval_jaxpr/vmap()/dot_general | solution.py:14
  292.1 13.6 %reshape.422 = bf16[40,12,64,128]{3,2,1,0:T(8,128)(2,1)} reshape(bf16[40,12,8192]{2,1,0:T(8,128)(2,1)} %convolution_convert_fusion.4) | data formatting | bytes 15728640 | tf_op jit(solution)/shard_map/while/body/eval_jaxpr/vmap()/reshape | solution.py:16
  305.7 7.0 %convolution_bitcast_fusion.4 = f32[40,64,64]{2,1,0:T(8,128)S(1)} fusion(bf16[40,12,64,128]{3,2,1,0:T(8,128)(2,1)} %reshape.422, bf16[4,12,64,128]{3,2,1,0:T(8,128)(2,1)S(1)} %get-tuple-element.199, s32[]{:T(128)} %get-tuple-element.187), kind=kOutput, calls=%fused_computation.11.clone.1.clone | convolution fusion | flops 503316480 | bytes 8716292 | tf_op jit(solution)/shard_map/while/body/eval_jaxpr/vmap(arc,asc->ars)/dot_general | solution.py:18
  (142 shorter events, 103.4 us)
Async XLA Ops:
  8.8 27.8 %all-to-all-start.2 = ((s32[8,1,2]{2,1,0:T(1,128)}), s32[8,1,2]{2,1,0:T(1,128)S(1)}, u32[]{:S(2)}, u32[]{:S(2)}) async-start(s32[8,1,2]{2,1,0:T(1,128)} %copy.144), calls=%async_computation.2 | async-start | bytes 8192 | tf_op jit(solution)/shard_map/all_to_all | solution.py:99
  15.1 66.9 %all-gather.3.cloned.1.call-start = ((), (), s32[]{:S(2)}) async-start(), calls=%async_computation.5 | async-start | bytes 3932160 | tf_op jit(solution)/shard_map/all_gather | solution.py:62
  18.3 4.1 %copy-start.3 = (bf16[4,4096]{1,0:T(4,128)(2,1)S(1)}, bf16[4,4096]{1,0:T(4,128)(2,1)}, u32[]{:S(2)}) copy-start(bf16[4,4096]{1,0:T(4,128)(2,1)} %param.11) | copy-start | bytes 98308
  18.3 5.5 %copy-start.7 = (s32[4,2]{0,1:T(2,128)S(1)}, s32[4,2]{0,1:T(2,128)}, u32[]{:S(2)}) copy-start(s32[4,2]{0,1:T(2,128)} %param.16) | copy-start | bytes 100
  18.4 6.6 %copy-start.4 = (s32[128,12]{0,1:T(8,128)S(1)}, s32[128,12]{0,1:T(8,128)}, u32[]{:S(2)}) copy-start(s32[128,12]{0,1:T(8,128)} %param.14) | copy-start | bytes 18436
  18.4 6.8 %copy-start.5 = (s32[4,2]{0,1:T(2,128)S(1)}, s32[4,2]{0,1:T(2,128)}, u32[]{:S(2)}) copy-start(s32[4,2]{0,1:T(2,128)} %param.15) | copy-start | bytes 100
  31.5 11.1 %copy-start.6 = (f32[4,64]{1,0:T(4,128)S(1)}, f32[4,64]{1,0:T(4,128)}, u32[]{:S(2)}) copy-start(f32[4,64]{1,0:T(4,128)} %param.12) | copy-start | bytes 3076
  31.6 20.9 %copy-start = (bf16[4,12,64,128]{3,2,1,0:T(8,128)(2,1)S(1)}, bf16[4,12,64,128]{3,2,1,0:T(8,128)(2,1)}, u32[]{:S(2)}) copy-start(bf16[4,12,64,128]{3,2,1,0:T(8,128)(2,1)} %broadcast_select_fusion.1) | copy-start | bytes 2359300
  36.6 10.9 %all-to-all-start = ((s32[8,1,2]{2,1,0:T(1,128)}), s32[8,1,2]{2,1,0:T(1,128)S(1)}, u32[]{:S(2)}, u32[]{:S(2)}) async-start(s32[8,1,2]{2,1,0:T(1,128)} %copy.140), calls=%async_computation | async-start | bytes 8192 | tf_op jit(solution)/shard_map/all_to_all | solution.py:98
  47.5 27.5 %all-to-all-start.4 = ((bf16[8,2,4096]{2,1,0:T(2,128)(2,1)}), bf16[8,2,4096]{2,1,0:T(2,128)(2,1)S(1)}, u32[]{:S(2)}, u32[]{:S(2)}) async-start(bf16[8,2,4096]{2,1,0:T(2,128)(2,1)} %broadcast_select_fusion.2), calls=%async_computation.4 | async-start | bytes 262144 | tf_op jit(solution)/shard_map/all_to_all | solution.py:109
  75.0 243.0 %all-to-all-start.1 = ((bf16[8,2,12,64,128]{4,3,2,1,0:T(8,128)(2,1)}), bf16[8,2,12,64,128]{4,3,2,1,0:T(8,128)(2,1)}, u32[]{:S(2)}, u32[]{:S(2)}) async-start(bf16[8,2,12,64,128]{4,3,2,1,0:T(8,128)(2,1)} %broadcast_select_fusion), calls=%async_computation.1 | async-start | bytes 6291456 | tf_op jit(solution)/shard_map/all_to_all | solution.py:108
  321.8 8.3 %copy-start.1 = (bf16[16,64,64]{2,1,0:T(8,128)(2,1)S(1)}, bf16[16,64,64]{2,1,0:T(8,128)(2,1)}, u32[]{:S(2)}) copy-start(bf16[16,64,64]{2,1,0:T(8,128)(2,1)} %reshape_reshape.3) | copy-start | bytes 393220
  324.1 12.2 %all-to-all-start.3 = ((f32[8,2,4096]{2,1,0:T(2,128)}), f32[8,2,4096]{2,1,0:T(2,128)S(1)}, u32[]{:S(2)}, u32[]{:S(2)}) async-start(f32[8,2,4096]{2,1,0:T(2,128)} %reshape.275), calls=%async_computation.3 | async-start | bytes 524288 | tf_op jit(solution)/shard_map/all_to_all | solution.py:127
  330.7 6.5 %copy-start.2 = (f32[4,64,64]{2,1,0:T(8,128)S(1)}, f32[4,64,64]{2,1,0:T(8,128)}, u32[]{:S(2)}) copy-start(f32[4,64,64]{2,1,0:T(8,128)} %reshape.280) | copy-start | bytes 196612
  330.7 6.5 %copy-start.8 = (f32[4,64,64]{2,0,1:T(4,128)S(1)}, f32[4,64,64]{2,0,1:T(4,128)}, u32[]{:S(2)}) copy-start(f32[4,64,64]{2,0,1:T(4,128)} %get-tuple-element.47) | copy-start | bytes 196612
Sparse Core Ops, SparseCore 0:
  18.1 29.9 all-gather.2
where the time goes:
time: 353 us; the launch traced here: 346 us
  local copies, waits for them, and re-layouts  184 us (52%)
  matrix products  92.5 us (26%)
  starting transfers between devices  29 us (8%)
  between operations  13.7 us (4%)
  other arithmetic  11.1 us (3%)
  waiting for transfers between devices  9.41 us (3%)
  blocking collectives  6.02 us (2%)
    reshape x5, local copies, waits for them, and re-layouts, intersection(): aligned = jnp.dot(matches, flat, preferred_element_type=jnp.float32).asty...  60.7 us
    reshape x5, local copies, waits for them, and re-layouts, intersection(): flat = right_coeff.reshape(right_coeff.shape[0], -1)  59.2 us
    dot_general x5, matrix products, intersection(): jnp.dot(matches, flat, preferred_element_type=jnp.float32)  48.4 us
    dot_general x5, matrix products, intersection(): jnp.einsum('arc,asc->ars', left_coeff, aligned, preferred_element_type=jn...  31.9 us
    gather x4, local copies, waits for them, and re-layouts, near_term(): group_coeff[chosen]  31.1 us
    dot_general x10, matrix products, carry_each(): jnp.einsum('kab,kbc,kdc->kad', intersections, square_amps(amplitude), int...  9.65 us
  transfers between devices with their start and end apart: 6, of which 2 were waited for; matrix products, arithmetic and copies ran while one was open for 80% of the time, Pallas kernels for 0%

commit v1 on v0

v1 whole, which is shorter than its diff:
```python
import functools

import jax
import jax.numpy as jnp
from jax import lax
from jax.experimental import pallas as pl
from jax.experimental.pallas import tpu as pltpu
from jax.sharding import PartitionSpec as P

NPNO = 64
NBLK = 32
ABSENT = 1 << 20
NOBODY = -(1 << 16)
EXT_ROWS = NPNO + 8
F32 = jnp.float32
BF16 = jnp.bfloat16
NT = (((1,), (1,)), ((), ()))
TN = (((0,), (0,)), ((), ()))


def split(value):
    high = value.astype(BF16)
    return high, (value - high.astype(F32)).astype(BF16)


def contract_kernel(p_slots, q_slots, near_rows, silent, pairs, blocks, meta, inv, near, *refs):
    count = (len(refs) - 9) // 2
    units, exts = refs[:count], refs[count : 2 * count]
    out, pool, dense, x_hi, x_lo, v_hi, v_lo, diag, sems = refs[2 * count :]
    per_unit = pairs * blocks
    rows = pairs * NPNO
    zero_at = count * per_unit
    copies = [
        pltpu.make_async_copy(units[u], pool.at[pl.ds(u * per_unit, per_unit)], sems.at[u])
        for u in range(count)
    ]
    for copy in copies:
        copy.start()
    pool[zero_at] = jnp.zeros(pool.shape[1:], BF16)
    diag[...] = jnp.zeros(diag.shape, BF16)
    waited = set()

    def arrive(u):
        if u not in waited:
            waited.add(u)
            copies[u].wait()

    def block_of(u, j, d):
        at = inv[(meta[1, u] + j) * NBLK + d] + (u * per_unit + j * blocks)
        return pool[jnp.minimum(at, zero_at)]

    for i, u in enumerate(p_slots):
        arrive(u)
        for j in range(pairs):
            for d in range(NBLK):
                dense[pl.ds(i * rows + j * NPNO, NPNO), pl.ds(d * 128, 128)] = block_of(u, j, d)

    lane = lax.broadcasted_iota(jnp.int32, (1, rows), 1)
    pair_of_lane = (lane // NPNO).astype(F32)
    left = lax.broadcasted_iota(jnp.int32, (NPNO, 128), 1) < NPNO
    for i, u in enumerate(q_slots):
        arrive(u)
        lhs = jnp.concatenate(
            [
                jnp.concatenate([block_of(u, j, d) for d in range(NBLK)], axis=1)
                for j in range(pairs)
            ],
            axis=0,
        )
        x = lax.dot_general(lhs, dense[...], NT, preferred_element_type=F32)
        xh, xl = split(x)
        here = pl.ds(i * rows, rows)
        x_hi[here, :] = xh
        x_lo[here, :] = xl
        for j in range(pairs):
            tile = exts[u][j // 2, :NPNO, :]
            keep = left if j % 2 == 0 else jnp.logical_not(left)
            diag[pl.ds(j * NPNO, NPNO), pl.ds((j // 2) * 128, 128)] = jnp.where(
                keep, tile.astype(F32), 0.0
            ).astype(BF16)
        amps = diag[...]
        v = jnp.dot(amps, xh, preferred_element_type=F32) + jnp.dot(
            amps, xl, preferred_element_type=F32
        )
        parts = []
        for n, s in enumerate(p_slots):
            p_id = meta[0, s].astype(F32) + pair_of_lane
            tails = [exts[s][h, NPNO:, :].astype(F32) for h in range(pairs // 2)]
            p_codes = [jnp.concatenate([t[k : k + 1] for t in tails], axis=1) for k in range(2)]
            strips = []
            for j in range(pairs):
                weight = jnp.zeros((1, rows), F32)
                if (u, s) not in silent:
                    q_id = (meta[0, u] + j).astype(F32)
                    q_tail = exts[u][j // 2, NPNO:, :].astype(F32)
                    for k in range(2):
                        at = 2 + 2 * (j % 2) + k
                        q_code = jnp.concatenate([q_tail[at : at + 1]] * (pairs // 2), axis=1)
                        weight = weight + jnp.where(q_code == p_id, 1.0, 0.0)
                        weight = weight + jnp.where(p_codes[k] == q_id, 1.0, 0.0)
                if n == 0 and u in near_rows:
                    at = near_rows[u] + j
                    weight = weight + near[at : at + 1, :]
                strips.append(
                    v[j * NPNO : (j + 1) * NPNO, n * rows : (n + 1) * rows] * weight
                )
            parts.append(jnp.concatenate(strips, axis=0))
        v = jnp.concatenate(parts, axis=1) if len(parts) > 1 else parts[0]
        vh, vl = split(v)
        v_hi[here, :] = vh
        v_lo[here, :] = vl

    row = lax.broadcasted_iota(jnp.int32, (rows, rows), 0) // NPNO
    col = lax.broadcasted_iota(jnp.int32, (rows, rows), 1) // NPNO
    own_block = row == col
    for i in range(len(p_slots)):
        cols = pl.ds(i * rows, rows)
        xh, xl, vh, vl = x_hi[:, cols], x_lo[:, cols], v_hi[:, cols], v_lo[:, cols]
        total = lax.dot_general(xh, vh, TN, preferred_element_type=F32)
        total += lax.dot_general(xh, vl, TN, preferred_element_type=F32)
        total += lax.dot_general(xl, vh, TN, preferred_element_type=F32)
        total = jnp.where(own_block, total, 0.0)
        for h in range(pairs // 2):
            two = total[h * 128 : (h + 1) * 128, h * 128 : (h + 1) * 128]
            out[i, h] = two[:NPNO] + two[NPNO:]


def contract(units, exts, meta, inv, near, p_slots, q_slots, near_rows=None, silent=()):
    near_rows = near_rows or {}
    count = len(units)
    pairs = exts[0].shape[0] * 2
    blocks = units[0].shape[0] // pairs
    rows = pairs * NPNO
    p_rows, q_rows = len(p_slots) * rows, len(q_slots) * rows
    smem = pl.BlockSpec(memory_space=pltpu.SMEM)
    vmem = pl.BlockSpec(memory_space=pltpu.VMEM)
    anywhere = pl.BlockSpec(memory_space=pl.ANY)
    body = functools.partial(
        contract_kernel, p_slots, q_slots, near_rows, frozenset(silent), pairs, blocks
    )
    flops = 2 * p_rows * q_rows * (NBLK * 128 + 5 * rows)
    return pl.pallas_call(
        body,
        out_shape=jax.ShapeDtypeStruct((len(p_slots), pairs // 2, NPNO, 128), F32),
        in_specs=[smem, smem, vmem] + [anywhere] * count + [vmem] * count,
        out_specs=vmem,
        scratch_shapes=[
            pltpu.VMEM((count * pairs * blocks + 1, NPNO, 128), BF16),
            pltpu.VMEM((p_rows, NBLK * 128), BF16),
            pltpu.VMEM((q_rows, p_rows), BF16),
            pltpu.VMEM((q_rows, p_rows), BF16),
            pltpu.VMEM((q_rows, p_rows), BF16),
            pltpu.VMEM((q_rows, p_rows), BF16),
            pltpu.VMEM((rows, rows), BF16),
            pltpu.SemaphoreType.DMA((count,)),
        ],
        cost_estimate=pl.CostEstimate(flops=flops, bytes_accessed=0, transcendentals=0),
        compiler_params=pltpu.CompilerParams(vmem_limit_bytes=48 << 20),
    )(meta, inv, near, *units, *exts)


def pack(square):
    pairs = square.shape[0]
    return (
        square.reshape(pairs // 2, 2, NPNO, NPNO).transpose(0, 2, 1, 3).reshape(pairs // 2, NPNO, 128)
    )


def unpack(packed):
    halves = packed.shape[0]
    return packed.reshape(halves, NPNO, 2, NPNO).transpose(0, 2, 1, 3).reshape(2 * halves, NPNO * NPNO)


def on_device(coeffs, amplitudes, denominators, pno_count, domains, far_owner, far_pair, near_pair):
    pairs, blocks = coeffs.shape[:2]
    occ_count = lax.axis_size("occ")
    rep_count = lax.axis_size("rep")
    occ = lax.axis_index("occ")
    rep = lax.axis_index("rep")
    live_rows = jnp.arange(NPNO, dtype=jnp.int32)[None, :] < pno_count[:, None]
    live_both = live_rows[:, :, None] & live_rows[:, None, :]
    amps = jnp.where(
        live_both, amplitudes.reshape(pairs, NPNO, NPNO), jnp.zeros((), BF16)
    )
    codes = (far_owner * pairs + far_pair + 1).astype(BF16).reshape(pairs // 2, 2, 2)
    ext = jnp.concatenate(
        [
            pack(amps),
            jnp.broadcast_to(
                codes.transpose(0, 2, 1)[..., None], (pairs // 2, 2, 2, NPNO)
            ).reshape(pairs // 2, 2, 128),
            jnp.broadcast_to(codes.reshape(pairs // 2, 4, 1), (pairs // 2, 4, 128)),
            jnp.zeros((pairs // 2, 2, 128), BF16),
        ],
        axis=1,
    )
    block_ids = jnp.arange(NBLK, dtype=jnp.int32)
    inv = jnp.min(
        jnp.where(
            domains[:, None, :] == block_ids[None, :, None],
            jnp.arange(blocks, dtype=jnp.int32)[None, None, :],
            ABSENT,
        ),
        axis=2,
    ).reshape(-1)
    own = coeffs.reshape(pairs * blocks, NPNO, 128)
    group_index = jnp.arange(rep_count * pairs, dtype=jnp.int32)
    slot_pair = ((group_index // pairs) ^ rep) * pairs + group_index % pairs
    near_weight = jnp.sum(
        (near_pair[None, :, :] == slot_pair[:, None, None]).astype(F32), axis=2
    )
    near = jnp.repeat(near_weight, NPNO, axis=1)
    base = pack(
        (denominators[:, :, None] + denominators[:, None, :]) * amps.astype(F32)
    )
    mask = pack(live_both.astype(F32))

    def pair_base(o, r):
        return (o * rep_count + r) * pairs

    def table(ids, bases):
        return jnp.stack([jnp.stack(ids), jnp.stack(bases)]).astype(jnp.int32)

    nobody = jnp.full((), NOBODY, jnp.int32)
    near_reps = [rep ^ k for k in range(rep_count)]

    if occ_count == 8 and rep_count == 4:
        layer, side = occ // 2, occ % 2
        inner = (layer == 1) | (layer == 2)
        end = jnp.where(layer < 2, 0, 3)
        occ_ids = [
            occ,
            end * 2 + side,
            (3 - layer) * 2 + side,
            layer * 2 + 1 - side,
            (3 - end) * 2 + side,
            end * 2 + 1 - side,
        ]
        ids = [occ * pairs + 1] + [
            jnp.where(inner, o * pairs + 1, nobody) for o in occ_ids[1:]
        ]
        bases = [pair_base(o, rep) for o in occ_ids]
        to_inner = [(s, 2 + s) for s in range(2)] + [(6 + s, 4 + s) for s in range(2)]
        from_inner = [(b, a) for a, b in to_inner]
        middle = [(a, a ^ 6) for a in range(2, 6)]
        across = [(a, a ^ 1) for a in range(2, 6)]
        swap_y = [(r, r ^ 2) for r in range(rep_count)]
        swap_core = [(r, r ^ 1) for r in range(rep_count)]
        both = (own, ext)

        def send(values, axis, perm):
            return tuple(lax.ppermute(v, axis, perm) for v in values)

        outer = send(both, "occ", to_inner)
        mid1 = send(both, "occ", middle)
        side1 = send(both, "occ", across)
        other_y = send(both, "rep", swap_y)
        other_core = send(both, "rep", swap_core)
        mid2 = send(outer, "occ", middle)
        side2 = send(outer, "occ", across)
        other_both = send(other_y, "rep", swap_core)

        def units_of(*items):
            return [u for u, _ in items], [e for _, e in items]

        first = contract(
            *units_of(both, outer, mid1, side1),
            table(ids[:4], bases[:4]),
            inv,
            near,
            (0, 1),
            (0, 1, 2, 3),
            near_rows={0: 0},
            silent=((1, 1),),
        )
        close = contract(
            *units_of(both, other_core, other_y, other_both),
            table([nobody] * 4, [pair_base(occ, r) for r in near_reps]),
            inv,
            near,
            (0,),
            (1, 2, 3),
            near_rows={k: k * pairs for k in range(1, 4)},
            silent=((1, 0), (2, 0), (3, 0)),
        )
        crossed = contract(
            *units_of(side1, side2, mid1, mid2),
            table([ids[3], ids[5], ids[2], ids[4]], [bases[3], bases[5], bases[2], bases[4]]),
            inv,
            near,
            (0, 1),
            (2, 3),
        )
        returned = lax.ppermute(crossed, "occ", across)
        last = contract(
            *units_of(both, outer, mid2, side2),
            table([ids[0], ids[1], ids[4], ids[5]], [bases[0], bases[1], bases[4], bases[5]]),
            inv,
            near,
            (0, 1),
            (2, 3),
        )
        total = first + last + returned
        home = lax.ppermute(total[1], "occ", from_inner)
        gain = total[0] + close[0] + home
    else:
        group_units = lax.all_gather(own, "rep", axis=0)
        group_exts = lax.all_gather(ext, "rep", axis=0)
        line_units = lax.all_gather(own, "occ", axis=0)
        line_exts = lax.all_gather(ext, "occ", axis=0)

        def add_near(total, k):
            r = rep ^ k
            rows = lax.dynamic_slice_in_dim(near, k * pairs, pairs, 0)
            part = contract(
                [own, group_units[r]],
                [ext, group_exts[r]],
                table([nobody, nobody], [pair_base(occ, rep), pair_base(occ, r)]),
                inv,
                rows,
                (0,),
                (1,),
                near_rows={1: 0},
                silent=((1, 0),),
            )
            return total + part[0], None

        def add_far(total, o):
            part = contract(
                [own, line_units[o]],
                [ext, line_exts[o]],
                table(
                    [occ * pairs + 1, o * pairs + 1], [pair_base(occ, rep), pair_base(o, rep)]
                ),
                inv,
                near,
                (0,),
                (1,),
            )
            return total + part[0], None

        gain = jnp.zeros(base.shape, F32)
        gain, _ = lax.scan(add_near, gain, jnp.arange(rep_count, dtype=jnp.int32))
        gain, _ = lax.scan(add_far, gain, jnp.arange(occ_count, dtype=jnp.int32))
    return unpack(jnp.where(mask > 0, base + gain, 0.0))


def solution(mesh):
    in_specs = (
        P(("occ", "rep"), None, None, None),
        P(("occ", "rep"), None),
        P(("occ", "rep"), None),
        P(("occ", "rep")),
        P(),
        P(("occ", "rep"), None),
        P(("occ", "rep"), None),
        P(("occ", "rep"), None),
    )
    out_specs = P(("occ", "rep"), None)
    return jax.shard_map(
        on_device, mesh=mesh, in_specs=in_specs, out_specs=out_specs, check_vma=False
    )
```

time: 353 us -> 81.8 us (0.23); the launches traced: 346 us -> 81.1 us
  local copies, waits for them, and re-layouts: 184 us -> 9.28 us
  matrix products: 92.5 us -> 0 us
  Pallas kernels: 0 us -> 27.1 us
  between operations: 13.7 us -> 0.48 us
  waiting for transfers between devices: 9.41 us -> 0.9 us
  starting transfers between devices: 29 us -> 35.7 us
  blocking collectives: 6.02 us -> 0 us
    reshape x20 -> x9, local copies, waits for them, and re-layouts: 125 us -> 2.3 us  [the longest x1 0.87 us: on_device(): amplitudes.reshape(pairs, NPNO, NPNO)]
    dot_general x25 -> x0, matrix products: 92.5 us -> none  [the longest x5 48.4 us: intersection(): jnp.dot(matches, flat, preferred_element_type=jnp.float32)]
    gather x20 -> x0, local copies, waits for them, and re-layouts: 45.9 us -> none  [the longest x4 31.1 us: near_term(): group_coeff[chosen]]
    ppermute x0 -> x18, starting transfers between devices: none -> 35.7 us  [the longest x16 30.7 us: send(): return tuple((lax.ppermute(v, axis, perm) for v in values))]
    all_to_all x5 -> x0, starting transfers between devices: 29 us -> none  [the longest x1 6.25 us: on_device(): lax.all_to_all(sources, 'occ', split_axis=0, concat_axis=0, tiled=True)]
    pallas_call x0 -> x4, Pallas kernels: none -> 27.1 us  [contract(): pl.pallas_call(body, out_shape=jax.ShapeDtypeStruct((len(p_slots), pairs...]
    select_n x11 -> x1, other arithmetic: 9.89 us -> 0.03 us  [on_device(): return unpack(jnp.where(mask > 0, base + gain, 0.0))]
    all_to_all x5 -> x0, waiting for transfers between devices: 9.39 us -> none  [the longest x1 4.84 us: on_device(): lax.all_to_all(targets, 'occ', split_axis=0, concat_axis=0, tiled=True)]
  transfers between devices with their start and end apart: 6 -> 18, of which waited for: 2 -> 1; matrix products, arithmetic and copies ran while one was open for 80% -> 14% of each run, Pallas kernels for 0% -> 33%
where the time goes in v1:
time: 81.8 us; the launch traced here: 81.1 us
  starting transfers between devices  35.7 us (44%)
  Pallas kernels  27.1 us (33%)
  local copies, waits for them, and re-layouts  9.28 us (11%)
  other arithmetic  7.61 us (9%)
  waiting for transfers between devices  0.9 us (1%)
    ppermute x16, starting transfers between devices, send(): return tuple((lax.ppermute(v, axis, perm) for v in values))  30.7 us
    pallas_call x4, Pallas kernels, contract(): pl.pallas_call(body, out_shape=jax.ShapeDtypeStruct((len(p_slots), pairs...  27.1 us
    unnamed x20, local copies, waits for them, and re-layouts  4.28 us
    ppermute x1, starting transfers between devices, on_device(): returned = lax.ppermute(crossed, 'occ', across)  3.63 us
    another operation x7, other arithmetic, table(): return jnp.stack([jnp.stack(ids), jnp.stack(bases)]).astype(jnp.int32)  2.03 us
  transfers between devices with their start and end apart: 18, of which 1 were waited for; matrix products, arithmetic and copies ran while one was open for 14% of the time, Pallas kernels for 33%

profile of v1, /device:TPU:8, one launch (start us, length us, event | category | flops | bytes accessed | tf_op | source)
XLA Modules:
  0.0 81.1 jit_solution(7027999441665334231)
XLA Ops:
  0.0 3.5 %collective-permute-start.2 = (bf16[48,64,128]{2,1,0:T(8,128)(2,1)}, bf16[48,64,128]{2,1,0:T(8,128)(2,1)S(1)}, u32[]{:S(2)}, u32[]{:S(2)}) collective-permute-start(bf16[48,64,128]{2,1,0:T(8,128)(2,1)} %bitcast.52), channel_id=1, source_target_pairs={{8,12},{12,8},{16,20},{20,16},{9,13},{13,9},{17,21},{21,17},{10,14... | collective-permute-start | bytes 2359304 | tf_op jit(solution)/shard_map/ppermute | solution.py:252
  3.5 1.3 %collective-permute-start = (bf16[48,64,128]{2,1,0:T(8,128)(2,1)}, bf16[48,64,128]{2,1,0:T(8,128)(2,1)S(1)}, u32[]{:S(2)}, u32[]{:S(2)}) collective-permute-start(bf16[48,64,128]{2,1,0:T(8,128)(2,1)} %bitcast.53), channel_id=1, source_target_pairs={{0,8},{4,12},{24,16},{28,20},{1,9},{5,13},{25,17},{29,21},{2,10},{... | collective-permute-start | bytes 2359304 | tf_op jit(solution)/shard_map/ppermute | solution.py:252
  4.8 3.5 %collective-permute-start.1 = (bf16[48,64,128]{2,1,0:T(8,128)(2,1)}, bf16[48,64,128]{2,1,0:T(8,128)(2,1)S(1)}, u32[]{:S(2)}, u32[]{:S(2)}) collective-permute-start(bf16[48,64,128]{2,1,0:T(8,128)(2,1)} %bitcast.54), channel_id=1, source_target_pairs={{8,16},{12,20},{16,8},{20,12},{9,17},{13,21},{17,9},{21,13},{10,18... | collective-permute-start | bytes 2359304 | tf_op jit(solution)/shard_map/ppermute | solution.py:252
  9.2 0.9 %reshape.124 = bf16[2,2,64,64]{3,2,1,0:T(8,128)(2,1)S(1)} reshape(bf16[4,4096]{1,0:T(4,128)(2,1)} %param.9) | data formatting | bytes 65536 | tf_op jit(solution)/shard_map/reshape | solution.py:183
  11.9 2.4 %collective-permute-start.5 = (bf16[2,72,128]{2,1,0:T(8,128)(2,1)S(1)}, bf16[2,72,128]{2,1,0:T(8,128)(2,1)S(1)}, u32[]{:S(2)}, u32[]{:S(2)}) collective-permute-start(bf16[2,72,128]{2,1,0:T(8,128)(2,1)S(1)} %maximum_maximum_fusion.refs_4_), channel_id=1, source_target_pairs={{8,12},{12,8},{16,20},{20,16},{9,13},{13,9},{17,21},{21,17},{10,14... | collective-permute-start | bytes 110600 | tf_op jit(solution)/shard_map/ppermute | solution.py:252
  14.3 1.3 %collective-permute-start.3 = (bf16[2,72,128]{2,1,0:T(8,128)(2,1)S(1)}, bf16[2,72,128]{2,1,0:T(8,128)(2,1)S(1)}, u32[]{:S(2)}, u32[]{:S(2)}) collective-permute-start(bf16[2,72,128]{2,1,0:T(8,128)(2,1)S(1)} %maximum_maximum_fusion.refs_4_), channel_id=1, source_target_pairs={{0,8},{4,12},{24,16},{28,20},{1,9},{5,13},{25,17},{29,21},{2,10},{... | collective-permute-start | bytes 110600 | tf_op jit(solution)/shard_map/ppermute | solution.py:252
  17.1 0.8 copy.25
  17.9 1.3 %select_reduce_fusion = s32[128,32]{0,1:T(8,128)} fusion(s32[128,12]{0,1:T(8,128)} %param.12), kind=kLoop, calls=%fused_computation.1 | loop fusion | flops 143360 | bytes 22528 | tf_op jit(solution)/shard_map/reduce_min | solution.py:198
  19.3 1.4 %convert_reduce_fusion = f32[16,4]{0,1:T(4,128)} fusion(s32[4,40]{1,0:T(4,128)} %param.15, s32[16]{0:T(128)S(1)} %fusion.4), kind=kLoop, calls=%fused_computation.13 | loop fusion | flops 7616 | bytes 960 | tf_op jit(solution)/shard_map/reduce_sum | solution.py:209
  20.7 1.0 %multiply_bitcast_fusion = f32[2,64,2,64]{3,2,1,0:T(2,128)S(1)} fusion(f32[2,2,64]{2,1,0:T(2,128)} %bitcast.63, f32[2,2,64]{1,2,0:T(8,128)S(1)} %copy.25, bf16[2,2,64,64]{3,2,1,0:T(8,128)(2,1)S(1)} %reshape.124, pred[2,2,64]{2,1,0:T(4,128)(4,1)S(1)} %iota_compare_fusion.1, pred[2,2,64]{1,2,0:T(8,128)(4,1)S(1)} %copy.26), kind=kLoop, calls=%fused_computation.4 | loop fusion | flops 81920 | bytes 100864 | tf_op jit(solution)/shard_map/transpose | solution.py:165
  23.1 2.7 %collective-permute-start.4 = (bf16[2,72,128]{2,1,0:T(8,128)(2,1)S(1)}, bf16[2,72,128]{2,1,0:T(8,128)(2,1)S(1)}, u32[]{:S(2)}, u32[]{:S(2)}) collective-permute-start(bf16[2,72,128]{2,1,0:T(8,128)(2,1)S(1)} %maximum_maximum_fusion.refs_4_), channel_id=1, source_target_pairs={{8,16},{12,20},{16,8},{20,12},{9,17},{13,21},{17,9},{21,13},{10,18... | collective-permute-start | bytes 110600 | tf_op jit(solution)/shard_map/ppermute | solution.py:252
  25.8 1.6 %collective-permute-start.15 = (bf16[2,72,128]{2,1,0:T(8,128)(2,1)S(1)}, bf16[2,72,128]{2,1,0:T(8,128)(2,1)S(1)}, u32[]{:S(2)}, u32[]{:S(2)}) collective-permute-start(bf16[2,72,128]{2,1,0:T(8,128)(2,1)S(1)} %maximum_maximum_fusion.refs_4_), channel_id=1, source_target_pairs={{0,2},{1,3},{2,0},{3,1},{4,6},{5,7},{6,4},{7,5},{8,10},{9,11},{10,... | collective-permute-start | bytes 110600 | tf_op jit(solution)/shard_map/ppermute | solution.py:252
  28.1 0.9 %collective-permute-done.4.refs_6_ = bf16[2,72,128]{2,1,0:T(8,128)(2,1)S(1)} collective-permute-done((bf16[2,72,128]{2,1,0:T(8,128)(2,1)S(1)}, bf16[2,72,128]{2,1,0:T(8,128)(2,1)S(1)}, u32[]{:S(2)}, u32[]{:S(2)}) %collective-permute-start.4) | collective-permute-done | bytes 36896 | tf_op jit(solution)/shard_map/ppermute | solution.py:252
  28.9 1.5 %collective-permute-start.12 = (bf16[48,64,128]{2,1,0:T(8,128)(2,1)S(1)}, bf16[48,64,128]{2,1,0:T(8,128)(2,1)}, u32[]{:S(2)}, u32[]{:S(2)}) collective-permute-start(bf16[48,64,128]{2,1,0:T(8,128)(2,1)S(1)} %bitcast.55), channel_id=1, source_target_pairs={{0,2},{1,3},{2,0},{3,1},{4,6},{5,7},{6,4},{7,5},{8,10},{9,11},{10,... | collective-permute-start | bytes 2359304 | tf_op jit(solution)/shard_map/ppermute | solution.py:252
  30.5 3.4 %collective-permute-start.7 = (bf16[48,64,128]{2,1,0:T(8,128)(2,1)S(1)}, bf16[48,64,128]{2,1,0:T(8,128)(2,1)}, u32[]{:S(2)}, u32[]{:S(2)}) collective-permute-start(bf16[48,64,128]{2,1,0:T(8,128)(2,1)S(1)} %collective-permute-done.refs_1_), channel_id=1, source_target_pairs={{8,12},{12,8},{16,20},{20,16},{9,13},{13,9},{17,21},{21,17},{10,14... | collective-permute-start | bytes 2359304 | tf_op jit(solution)/shard_map/ppermute | solution.py:252
  33.9 2.7 %collective-permute-start.6 = (bf16[48,64,128]{2,1,0:T(8,128)(2,1)S(1)}, bf16[48,64,128]{2,1,0:T(8,128)(2,1)}, u32[]{:S(2)}, u32[]{:S(2)}) collective-permute-start(bf16[48,64,128]{2,1,0:T(8,128)(2,1)S(1)} %collective-permute-done.refs_1_), channel_id=1, source_target_pairs={{8,16},{12,20},{16,8},{20,12},{9,17},{13,21},{17,9},{21,13},{10,18... | collective-permute-start | bytes 2359304 | tf_op jit(solution)/shard_map/ppermute | solution.py:252
  41.0 2.4 %collective-permute-start.9 = (bf16[2,72,128]{2,1,0:T(8,128)(2,1)S(1)}, bf16[2,72,128]{2,1,0:T(8,128)(2,1)S(1)}, u32[]{:S(2)}, u32[]{:S(2)}) collective-permute-start(bf16[2,72,128]{2,1,0:T(8,128)(2,1)S(1)} %collective-permute-done.3.refs_5_), channel_id=1, source_target_pairs={{8,12},{12,8},{16,20},{20,16},{9,13},{13,9},{17,21},{21,17},{10,14... | collective-permute-start | bytes 110600 | tf_op jit(solution)/shard_map/ppermute | solution.py:252
  43.5 3.3 %collective-permute-start.8 = (bf16[2,72,128]{2,1,0:T(8,128)(2,1)S(1)}, bf16[2,72,128]{2,1,0:T(8,128)(2,1)S(1)}, u32[]{:S(2)}, u32[]{:S(2)}) collective-permute-start(bf16[2,72,128]{2,1,0:T(8,128)(2,1)S(1)} %collective-permute-done.3.refs_5_), channel_id=1, source_target_pairs={{8,16},{12,20},{16,8},{20,12},{9,17},{13,21},{17,9},{21,13},{10,18... | collective-permute-start | bytes 110600 | tf_op jit(solution)/shard_map/ppermute | solution.py:252
  46.8 8.6 %shard_map.82 = f32[2,2,64,128]{3,2,1,0:T(8,128)S(1)} custom-call(s32[2,4]{1,0:T(2,128)S(1)} %pad_add_fusion.meta, s32[4096]{0:T(1024)S(1)} %reshape.126.inv, f32[16,256]{1,0:T(8,128)S(1)} %reshape.127.near, bf16[48,64,128]{2,1,0:T(8,128)(2,1)S(1)} %bitcast.56, bf16[48,64,128]{2,1,0:T(8,128)(2,1)S(1)} %collective-permute-done.refs_1_, ...), custom_call_target="tpu_custom_call" | custom-call | flops 5637144576 | tf_op jit(solution)/shard_map/pallas_call | solution.py:142
  56.5 6.2 %shard_map.84 = f32[2,2,64,128]{3,2,1,0:T(8,128)S(1)} custom-call(s32[2,4]{1,0:T(2,128)S(1)} %pad_add_fusion.2.meta, s32[4096]{0:T(1024)S(1)} %reshape.126.inv, f32[16,256]{1,0:T(8,128)S(1)} %reshape.127.near, bf16[48,64,128]{2,1,0:T(8,128)(2,1)S(1)} %collective-permute-done.2.refs_3_.refs_0_, bf16[48,64,128]{2,1,0:T(8,128)(2,1)} %collective-permute-done.7.refs_3_.refs_1_, ...), custom_call_target="tpu_custom_call" | custom-call | flops 2818572288 | tf_op jit(solution)/shard_map/pallas_call | solution.py:142
  62.7 3.6 %collective-permute-start.10 = (f32[2,2,64,128]{3,2,1,0:T(8,128)S(1)}, f32[2,2,64,128]{3,2,1,0:T(8,128)S(1)}, u32[]{:S(2)}, u32[]{:S(2)}) collective-permute-start(f32[2,2,64,128]{3,2,1,0:T(8,128)S(1)} %shard_map.84), channel_id=1, source_target_pairs={{8,12},{12,8},{16,20},{20,16},{9,13},{13,9},{17,21},{21,17},{10,14... | collective-permute-start | bytes 393224 | tf_op jit(solution)/shard_map/ppermute | solution.py:294
  66.4 5.7 %shard_map.83 = f32[2,2,64,128]{3,2,1,0:T(8,128)S(1)} custom-call(s32[2,4]{1,0:T(2,128)S(1)} %pad_add_fusion.1.meta, s32[4096]{0:T(1024)S(1)} %reshape.126.inv, f32[16,256]{1,0:T(8,128)S(1)} %reshape.127.near, bf16[48,64,128]{2,1,0:T(8,128)(2,1)S(1)} %bitcast.58, bf16[48,64,128]{2,1,0:T(8,128)(2,1)S(1)} %collective-permute-done.refs_1_, ...), custom_call_target="tpu_custom_call" | custom-call | flops 2818572288 | tf_op jit(solution)/shard_map/pallas_call | solution.py:142
  72.2 1.3 %collective-permute-start.17 = (f32[2,64,128]{2,1,0:T(8,128)S(1)}, f32[2,64,128]{2,1,0:T(8,128)S(1)}, u32[]{:S(2)}, u32[]{:S(2)}) collective-permute-start(f32[2,64,128]{2,1,0:T(8,128)S(1)} %slice_bitcast_fusion), channel_id=1, source_target_pairs={{8,0},{12,4},{16,24},{20,28},{9,1},{13,5},{17,25},{21,29},{10,2},{... | collective-permute-start | bytes 196616 | tf_op jit(solution)/shard_map/ppermute | solution.py:304
  73.5 6.6 %shard_map.85 = f32[1,2,64,128]{3,2,1,0:T(8,128)S(1)} custom-call(s32[2,4]{1,0:T(2,128)S(1)} %stack.144.meta, s32[4096]{0:T(1024)S(1)} %reshape.126.inv, f32[16,256]{1,0:T(8,128)S(1)} %reshape.127.near, bf16[48,64,128]{2,1,0:T(8,128)(2,1)S(1)} %bitcast.59, bf16[48,64,128]{2,1,0:T(8,128)(2,1)S(1)} %collective-permute-done.11.refs_1_, ...), custom_call_target="tpu_custom_call" | custom-call | flops 2113929216 | tf_op jit(solution)/shard_map/pallas_call | solution.py:142
  (86 shorter events, 12.6 us)
Async XLA Ops:
  0.0 28.9 %copy-start = (bf16[4,12,64,128]{3,2,1,0:T(8,128)(2,1)S(1)}, bf16[4,12,64,128]{3,2,1,0:T(8,128)(2,1)}, u32[]{:S(2)}) copy-start(bf16[4,12,64,128]{3,2,1,0:T(8,128)(2,1)} %param.8) | copy-start | bytes 2359300
  0.0 41.0 %collective-permute-start.2 = (bf16[48,64,128]{2,1,0:T(8,128)(2,1)}, bf16[48,64,128]{2,1,0:T(8,128)(2,1)S(1)}, u32[]{:S(2)}, u32[]{:S(2)}) collective-permute-start(bf16[48,64,128]{2,1,0:T(8,128)(2,1)} %bitcast.52), channel_id=1, source_target_pairs={{8,12},{12,8},{16,20},{20,16},{9,13},{13,9},{17,21},{21,17},{10,14... | collective-permute-start | bytes 2359304 | tf_op jit(solution)/shard_map/ppermute | solution.py:252
  3.5 26.9 %collective-permute-start = (bf16[48,64,128]{2,1,0:T(8,128)(2,1)}, bf16[48,64,128]{2,1,0:T(8,128)(2,1)S(1)}, u32[]{:S(2)}, u32[]{:S(2)}) collective-permute-start(bf16[48,64,128]{2,1,0:T(8,128)(2,1)} %bitcast.53), channel_id=1, source_target_pairs={{0,8},{4,12},{24,16},{28,20},{1,9},{5,13},{25,17},{29,21},{2,10},{... | collective-permute-start | bytes 2359304 | tf_op jit(solution)/shard_map/ppermute | solution.py:252
  4.8 38.6 %collective-permute-start.1 = (bf16[48,64,128]{2,1,0:T(8,128)(2,1)}, bf16[48,64,128]{2,1,0:T(8,128)(2,1)S(1)}, u32[]{:S(2)}, u32[]{:S(2)}) collective-permute-start(bf16[48,64,128]{2,1,0:T(8,128)(2,1)} %bitcast.54), channel_id=1, source_target_pairs={{8,16},{12,20},{16,8},{20,12},{9,17},{13,21},{17,9},{21,13},{10,18... | collective-permute-start | bytes 2359304 | tf_op jit(solution)/shard_map/ppermute | solution.py:252
  10.8 11.6 %copy-start.2 = (s32[2,2]{1,0:T(2,128)}, s32[2,2]{1,0:T(2,128)S(1)}, u32[]{:S(2)}) copy-start(s32[2,2]{1,0:T(2,128)S(1)} %lt.57) | copy-start | bytes 52
  11.9 11.2 %collective-permute-start.5 = (bf16[2,72,128]{2,1,0:T(8,128)(2,1)S(1)}, bf16[2,72,128]{2,1,0:T(8,128)(2,1)S(1)}, u32[]{:S(2)}, u32[]{:S(2)}) collective-permute-start(bf16[2,72,128]{2,1,0:T(8,128)(2,1)S(1)} %maximum_maximum_fusion.refs_4_), channel_id=1, source_target_pairs={{8,12},{12,8},{16,20},{20,16},{9,13},{13,9},{17,21},{21,17},{10,14... | collective-permute-start | bytes 110600 | tf_op jit(solution)/shard_map/ppermute | solution.py:252
  14.3 11.5 %collective-permute-start.3 = (bf16[2,72,128]{2,1,0:T(8,128)(2,1)S(1)}, bf16[2,72,128]{2,1,0:T(8,128)(2,1)S(1)}, u32[]{:S(2)}, u32[]{:S(2)}) collective-permute-start(bf16[2,72,128]{2,1,0:T(8,128)(2,1)S(1)} %maximum_maximum_fusion.refs_4_), channel_id=1, source_target_pairs={{0,8},{4,12},{24,16},{28,20},{1,9},{5,13},{25,17},{29,21},{2,10},{... | collective-permute-start | bytes 110600 | tf_op jit(solution)/shard_map/ppermute | solution.py:252
  23.1 5.9 %collective-permute-start.4 = (bf16[2,72,128]{2,1,0:T(8,128)(2,1)S(1)}, bf16[2,72,128]{2,1,0:T(8,128)(2,1)S(1)}, u32[]{:S(2)}, u32[]{:S(2)}) collective-permute-start(bf16[2,72,128]{2,1,0:T(8,128)(2,1)S(1)} %maximum_maximum_fusion.refs_4_), channel_id=1, source_target_pairs={{8,16},{12,20},{16,8},{20,12},{9,17},{13,21},{17,9},{21,13},{10,18... | collective-permute-start | bytes 110600 | tf_op jit(solution)/shard_map/ppermute | solution.py:252
  25.8 8.1 %collective-permute-start.15 = (bf16[2,72,128]{2,1,0:T(8,128)(2,1)S(1)}, bf16[2,72,128]{2,1,0:T(8,128)(2,1)S(1)}, u32[]{:S(2)}, u32[]{:S(2)}) collective-permute-start(bf16[2,72,128]{2,1,0:T(8,128)(2,1)S(1)} %maximum_maximum_fusion.refs_4_), channel_id=1, source_target_pairs={{0,2},{1,3},{2,0},{3,1},{4,6},{5,7},{6,4},{7,5},{8,10},{9,11},{10,... | collective-permute-start | bytes 110600 | tf_op jit(solution)/shard_map/ppermute | solution.py:252
  27.4 0.7 copy-start.6
  27.4 0.7 copy-start.7
  28.9 27.1 %collective-permute-start.12 = (bf16[48,64,128]{2,1,0:T(8,128)(2,1)S(1)}, bf16[48,64,128]{2,1,0:T(8,128)(2,1)}, u32[]{:S(2)}, u32[]{:S(2)}) collective-permute-start(bf16[48,64,128]{2,1,0:T(8,128)(2,1)S(1)} %bitcast.55), channel_id=1, source_target_pairs={{0,2},{1,3},{2,0},{3,1},{4,6},{5,7},{6,4},{7,5},{8,10},{9,11},{10,... | collective-permute-start | bytes 2359304 | tf_op jit(solution)/shard_map/ppermute | solution.py:252
  30.5 25.7 %collective-permute-start.7 = (bf16[48,64,128]{2,1,0:T(8,128)(2,1)S(1)}, bf16[48,64,128]{2,1,0:T(8,128)(2,1)}, u32[]{:S(2)}, u32[]{:S(2)}) collective-permute-start(bf16[48,64,128]{2,1,0:T(8,128)(2,1)S(1)} %collective-permute-done.refs_1_), channel_id=1, source_target_pairs={{8,12},{12,8},{16,20},{20,16},{9,13},{13,9},{17,21},{21,17},{10,14... | collective-permute-start | bytes 2359304 | tf_op jit(solution)/shard_map/ppermute | solution.py:252
  33.9 22.7 %collective-permute-start.6 = (bf16[48,64,128]{2,1,0:T(8,128)(2,1)S(1)}, bf16[48,64,128]{2,1,0:T(8,128)(2,1)}, u32[]{:S(2)}, u32[]{:S(2)}) collective-permute-start(bf16[48,64,128]{2,1,0:T(8,128)(2,1)S(1)} %collective-permute-done.refs_1_), channel_id=1, source_target_pairs={{8,16},{12,20},{16,8},{20,12},{9,17},{13,21},{17,9},{21,13},{10,18... | collective-permute-start | bytes 2359304 | tf_op jit(solution)/shard_map/ppermute | solution.py:252
  37.1 0.7 copy-start.1
  38.0 0.7 copy-start.4
  41.0 14.4 %collective-permute-start.9 = (bf16[2,72,128]{2,1,0:T(8,128)(2,1)S(1)}, bf16[2,72,128]{2,1,0:T(8,128)(2,1)S(1)}, u32[]{:S(2)}, u32[]{:S(2)}) collective-permute-start(bf16[2,72,128]{2,1,0:T(8,128)(2,1)S(1)} %collective-permute-done.3.refs_5_), channel_id=1, source_target_pairs={{8,12},{12,8},{16,20},{20,16},{9,13},{13,9},{17,21},{21,17},{10,14... | collective-permute-start | bytes 110600 | tf_op jit(solution)/shard_map/ppermute | solution.py:252
  43.5 12.0 %collective-permute-start.8 = (bf16[2,72,128]{2,1,0:T(8,128)(2,1)S(1)}, bf16[2,72,128]{2,1,0:T(8,128)(2,1)S(1)}, u32[]{:S(2)}, u32[]{:S(2)}) collective-permute-start(bf16[2,72,128]{2,1,0:T(8,128)(2,1)S(1)} %collective-permute-done.3.refs_5_), channel_id=1, source_target_pairs={{8,16},{12,20},{16,8},{20,12},{9,17},{13,21},{17,9},{21,13},{10,18... | collective-permute-start | bytes 110600 | tf_op jit(solution)/shard_map/ppermute | solution.py:252
  55.4 18.0 %collective-permute-start.11 = (bf16[48,64,128]{2,1,0:T(8,128)(2,1)S(1)}, bf16[48,64,128]{2,1,0:T(8,128)(2,1)S(1)}, u32[]{:S(2)}, u32[]{:S(2)}) collective-permute-start(bf16[48,64,128]{2,1,0:T(8,128)(2,1)S(1)} %bitcast.57), channel_id=1, source_target_pairs={{0,1},{1,0},{2,3},{3,2},{4,5},{5,4},{6,7},{7,6},{8,9},{9,8},{10,11... | collective-permute-start | bytes 2359304 | tf_op jit(solution)/shard_map/ppermute | solution.py:252
  55.5 17.9 %collective-permute-start.14 = (bf16[2,72,128]{2,1,0:T(8,128)(2,1)S(1)}, bf16[2,72,128]{2,1,0:T(8,128)(2,1)S(1)}, u32[]{:S(2)}, u32[]{:S(2)}) collective-permute-start(bf16[2,72,128]{2,1,0:T(8,128)(2,1)S(1)} %maximum_maximum_fusion.refs_4_), channel_id=1, source_target_pairs={{0,1},{1,0},{2,3},{3,2},{4,5},{5,4},{6,7},{7,6},{8,9},{9,8},{10,11... | collective-permute-start | bytes 110600 | tf_op jit(solution)/shard_map/ppermute | solution.py:252
  56.0 17.4 %collective-permute-start.16 = (bf16[2,72,128]{2,1,0:T(8,128)(2,1)S(1)}, bf16[2,72,128]{2,1,0:T(8,128)(2,1)S(1)}, u32[]{:S(2)}, u32[]{:S(2)}) collective-permute-start(bf16[2,72,128]{2,1,0:T(8,128)(2,1)S(1)} %collective-permute-done.15.refs_6_), channel_id=1, source_target_pairs={{0,1},{1,0},{2,3},{3,2},{4,5},{5,4},{6,7},{7,6},{8,9},{9,8},{10,11... | collective-permute-start | bytes 110600 | tf_op jit(solution)/shard_map/ppermute | solution.py:252
  56.1 17.4 %collective-permute-start.13 = (bf16[48,64,128]{2,1,0:T(8,128)(2,1)}, bf16[48,64,128]{2,1,0:T(8,128)(2,1)S(1)}, u32[]{:S(2)}, u32[]{:S(2)}) collective-permute-start(bf16[48,64,128]{2,1,0:T(8,128)(2,1)} %collective-permute-done.12.refs_2_), channel_id=1, source_target_pairs={{0,1},{1,0},{2,3},{3,2},{4,5},{5,4},{6,7},{7,6},{8,9},{9,8},{10,11... | collective-permute-start | bytes 2359304 | tf_op jit(solution)/shard_map/ppermute | solution.py:252
  62.7 9.4 %collective-permute-start.10 = (f32[2,2,64,128]{3,2,1,0:T(8,128)S(1)}, f32[2,2,64,128]{3,2,1,0:T(8,128)S(1)}, u32[]{:S(2)}, u32[]{:S(2)}) collective-permute-start(f32[2,2,64,128]{3,2,1,0:T(8,128)S(1)} %shard_map.84), channel_id=1, source_target_pairs={{8,12},{12,8},{16,20},{20,16},{9,13},{13,9},{17,21},{21,17},{10,14... | collective-permute-start | bytes 393224 | tf_op jit(solution)/shard_map/ppermute | solution.py:294
  72.2 8.0 %collective-permute-start.17 = (f32[2,64,128]{2,1,0:T(8,128)S(1)}, f32[2,64,128]{2,1,0:T(8,128)S(1)}, u32[]{:S(2)}, u32[]{:S(2)}) collective-permute-start(f32[2,64,128]{2,1,0:T(8,128)S(1)} %slice_bitcast_fusion), channel_id=1, source_target_pairs={{8,0},{12,4},{16,24},{20,28},{9,1},{13,5},{17,25},{21,29},{10,2},{... | collective-permute-start | bytes 196616 | tf_op jit(solution)/shard_map/ppermute | solution.py:304
  (4 other events, 2.6 us)

commit v2 on v0

v2 whole, which is shorter than its diff:
```python
import functools

import jax
import jax.numpy as jnp
from jax import lax
from jax.experimental import pallas as pl
from jax.experimental.pallas import tpu as pltpu
from jax.sharding import PartitionSpec as P


NPNO = 64
NBLK = 32
ABSENT = 1 << 10
GRANT = 16 << 20
NOBODY = -(1 << 16)
F32 = jnp.float32
BF16 = jnp.bfloat16
NT = (((1,), (1,)), ((), ()))
TN = (((0,), (0,)), ((), ()))


def split(value):
    high = value.astype(BF16)
    return high, (value - high.astype(F32)).astype(BF16)


def contract_kernel(plan, ready, raw, kept, added, closing, pairs, blocks, places, ints, chosen, energies, *refs):
    p_slots, plan, near_slots, silent, inner_only = plan
    ids_at, bases_at, inner_at, rep_at, count_at = places
    slots = sorted(ready + raw)
    near_at, meta_at = ints.shape[0] - 1 - pairs, ints.shape[0] - 1
    refs = list(refs)

    def take(names):
        return {name: refs.pop(0) for name in names}

    dense = take(ready)
    units = take(raw)
    exts = take(slots)
    addends = take(added)
    outs = take(p_slots)
    shown = refs.pop(0) if closing else None
    dense.update(take(kept))
    dense.update(take([u for u in raw if u not in kept]))
    x_hi, x_lo, v_hi, v_lo, diag, near, inv = refs
    rows = pairs * NPNO
    halves = pairs // 2
    inner = ints[meta_at, inner_at].astype(F32)
    for n, u in enumerate(raw):
        for j in range(pairs):
            here = (n * pairs + j) * NBLK
            for d in range(NBLK):
                inv[here + d] = ABSENT
            for a in range(blocks):
                inv[here + ints[a, ints[meta_at, bases_at + u] + j]] = a
    for n, u in enumerate(raw):
        for j in range(pairs):
            for d in range(NBLK):
                at = inv[(n * pairs + j) * NBLK + d]
                block = units[u][j * blocks + (at & (ABSENT - 1))]
                dense[u][pl.ds(j * NPNO, NPNO), pl.ds(d * 128, 128)] = jnp.where(
                    at < ABSENT, block, jnp.zeros((), BF16)
                )
    diag[...] = jnp.zeros(diag.shape, BF16)
    lane = lax.broadcasted_iota(jnp.int32, (1, rows), 1)
    pair_of_lane = (lane // NPNO).astype(F32)
    left = lax.broadcasted_iota(jnp.int32, (NPNO, 128), 1) < NPNO
    if near_slots:
        group = near.shape[0]
        members = lax.broadcasted_iota(jnp.int32, (group, chosen.shape[1]), 0)
        lanes = lax.broadcasted_iota(jnp.int32, (group, rows), 1) // NPNO
        times = jnp.zeros((group, rows), F32)
        for j in range(pairs):
            hits = jnp.where(chosen[near_at + j : near_at + j + 1, :] == members, 1.0, 0.0)
            times = jnp.where(lanes == j, jnp.sum(hits, axis=1, keepdims=True), times)
        near[...] = times
    q_slots = sorted({q for q, _ in plan})
    for n, u in enumerate(q_slots):
        for j in range(pairs):
            tile = exts[u][j // 2, :NPNO, :]
            keep = left if j % 2 == 0 else jnp.logical_not(left)
            diag[n, pl.ds(j * NPNO, NPNO), pl.ds((j // 2) * 128, 128)] = jnp.where(
                keep, tile, jnp.zeros((), BF16)
            )

    row = lax.broadcasted_iota(jnp.int32, (rows, rows), 0) // NPNO
    col = lax.broadcasted_iota(jnp.int32, (rows, rows), 1) // NPNO
    own_block = row == col
    spots = {block: pl.ds(n * rows, rows) for n, block in enumerate(plan)}
    for u, s in plan:
        x = lax.dot_general(dense[u][...], dense[s][...], NT, preferred_element_type=F32)
        x_hi[spots[u, s], :], x_lo[spots[u, s], :] = split(x)
    for u, s in plan:
        here = spots[u, s]
        amps = diag[q_slots.index(u)]
        v = jnp.dot(amps, x_hi[here, :], preferred_element_type=F32)
        v += jnp.dot(amps, x_lo[here, :], preferred_element_type=F32)
        p_id = ints[meta_at, ids_at + s].astype(F32) + pair_of_lane
        tails = [exts[s][h, NPNO:, :].astype(F32) for h in range(halves)]
        p_codes = [jnp.concatenate([t[k : k + 1] for t in tails], axis=1) for k in range(2)]
        strips = []
        for j in range(pairs):
            weight = jnp.zeros((1, rows), F32)
            if (u, s) not in silent:
                q_id = (ints[meta_at, ids_at + u] + j).astype(F32)
                q_tail = exts[u][j // 2, NPNO:, :].astype(F32)
                for k in range(2):
                    at = 2 + 2 * (j % 2) + k
                    q_code = jnp.concatenate([q_tail[at : at + 1]] * halves, axis=1)
                    weight = weight + jnp.where(q_code == p_id, 1.0, 0.0)
                    weight = weight + jnp.where(p_codes[k] == q_id, 1.0, 0.0)
                if (u, s) in inner_only:
                    weight = weight * inner
            if u in near_slots and s == p_slots[0]:
                at = (ints[meta_at, rep_at] ^ near_slots[u]) * pairs + j
                weight = weight + near[pl.ds(at, 1), :]
            strips.append(v[j * NPNO : (j + 1) * NPNO] * weight)
        v_hi[here, :], v_lo[here, :] = split(jnp.concatenate(strips, axis=0))
    for s in p_slots:
        mine = [n for n, block in enumerate(plan) if block[1] == s]
        deep = pl.ds(mine[0] * rows, len(mine) * rows)
        xh, xl, vh, vl = x_hi[deep, :], x_lo[deep, :], v_hi[deep, :], v_lo[deep, :]
        total = lax.dot_general(xh, vh, TN, preferred_element_type=F32)
        total += lax.dot_general(xh, vl, TN, preferred_element_type=F32)
        total += lax.dot_general(xl, vh, TN, preferred_element_type=F32)
        total = jnp.where(own_block, total, 0.0)
        for h in range(halves):
            two = total[h * 128 : (h + 1) * 128, h * 128 : (h + 1) * 128]
            two = two[:NPNO] + two[NPNO:]
            if s in added:
                two = two + addends[s][h]
            if closing:
                even, odd = energies[2 * h : 2 * h + 1, :], energies[2 * h + 1 : 2 * h + 2, :]
                a = lax.broadcasted_iota(jnp.int32, (NPNO, 128), 0)
                b = lax.broadcasted_iota(jnp.int32, (NPNO, 128), 1)
                down = [
                    jnp.sum(jnp.where(a == b, e, 0.0), axis=1, keepdims=True) for e in (even, odd)
                ]
                both = jnp.where(left, even, odd) + jnp.where(left, *down)
                two = two + both * exts[s][h, :NPNO, :].astype(F32)
                live = jnp.where(
                    left, ints[meta_at, count_at + 2 * h], ints[meta_at, count_at + 2 * h + 1]
                )
                seen = jnp.logical_and(a < live, jnp.where(left, b, b - NPNO) < live)
                shown[h] = jnp.where(seen, 1.0, 0.0)
            outs[s][h] = two


def contract(
    dense,
    units,
    exts,
    small,
    places,
    plan,
    kept=(),
    addends=None,
    closing=False,
    near_slots=None,
    silent=(),
    inner_only=(),
):
    ready, raw = sorted(dense), sorted(units)
    slots = sorted(ready + raw)
    kept = sorted(kept)
    p_slots = sorted({p for _, p in plan})
    plan = sorted(plan, key=lambda block: block[1])
    pairs = exts[slots[0]].shape[0] * 2
    addends = addends or {}
    added = sorted(addends)
    blocks = units[raw[0]].shape[0] // pairs if raw else 0
    rows = pairs * NPNO
    deep = rows * len(plan)
    group = lax.axis_size("rep") * pairs
    wide = NBLK * 128
    smem = pl.BlockSpec(memory_space=pltpu.SMEM)
    vmem = pl.BlockSpec(memory_space=pltpu.VMEM)
    plan = (p_slots, plan, near_slots or {}, frozenset(silent), frozenset(inner_only))
    body = functools.partial(
        contract_kernel, plan, ready, raw, kept, added, closing, pairs, blocks, places
    )
    q_count = len({q for q, _ in plan[1]})
    results = pl.pallas_call(
        body,
        out_shape=[jax.ShapeDtypeStruct((pairs // 2, NPNO, 128), F32)] * (len(p_slots) + closing)
        + [jax.ShapeDtypeStruct((rows, wide), BF16)] * len(kept),
        in_specs=[smem, vmem, vmem] + [vmem] * (2 * len(slots) + len(added)),
        out_specs=[vmem] * (len(p_slots) + closing + len(kept)),
        scratch_shapes=[pltpu.VMEM((rows, wide), BF16)] * (len(raw) - len(kept))
        + [pltpu.VMEM((deep, rows), BF16)] * 4
        + [
            pltpu.VMEM((q_count, rows, rows), BF16),
            pltpu.VMEM((group, rows), F32),
            pltpu.SMEM((max(1, len(raw)) * pairs * NBLK,), jnp.int32),
        ],
        cost_estimate=pl.CostEstimate(
            flops=2 * deep * rows * (wide + 5 * rows), bytes_accessed=0, transcendentals=0
        ),
        compiler_params=pltpu.CompilerParams(vmem_limit_bytes=GRANT),
    )(
        *small,
        *[dense[u] for u in ready],
        *[units[u] for u in raw],
        *[exts[u] for u in slots],
        *[addends[s] for s in added],
    )
    sums = dict(zip(p_slots, results))
    if closing:
        sums["shown"] = results[len(p_slots)]
    return sums, dict(zip(kept, results[len(p_slots) + closing :]))


def pack(square):
    pairs = square.shape[0]
    return (
        square.reshape(pairs // 2, 2, NPNO, NPNO).transpose(0, 2, 1, 3).reshape(pairs // 2, NPNO, 128)
    )


def unpack(packed):
    halves = packed.shape[0]
    return packed.reshape(halves, NPNO, 2, NPNO).transpose(0, 2, 1, 3).reshape(2 * halves, NPNO * NPNO)


def residual_of(coeffs, amplitudes, denominators, pno_count, domains, far_owner, far_pair, near_pair):
    pairs, blocks = coeffs.shape[:2]
    occ_count = lax.axis_size("occ")
    rep_count = lax.axis_size("rep")
    occ = lax.axis_index("occ")
    rep = lax.axis_index("rep")
    live_rows = jnp.arange(NPNO, dtype=jnp.int32)[None, :] < pno_count[:, None]
    live_both = live_rows[:, :, None] & live_rows[:, None, :]
    amps = jnp.where(
        live_both, amplitudes.reshape(pairs, NPNO, NPNO), jnp.zeros((), BF16)
    )
    codes = (far_owner * pairs + far_pair + 1).astype(BF16).reshape(pairs // 2, 2, 2)
    ext = jnp.concatenate(
        [
            pack(amps),
            jnp.broadcast_to(
                codes.transpose(0, 2, 1)[..., None], (pairs // 2, 2, 2, NPNO)
            ).reshape(pairs // 2, 2, 128),
            jnp.broadcast_to(codes.reshape(pairs // 2, 4, 1), (pairs // 2, 4, 128)),
            jnp.zeros((pairs // 2, 2, 128), BF16),
        ],
        axis=1,
    )
    own = coeffs.reshape(pairs * blocks, NPNO, 128)
    nobody = jnp.full((), NOBODY, jnp.int32)

    energies = jnp.concatenate([denominators, denominators], axis=1)

    def small_of(ids, bases, inner, rep_now):
        values = [jnp.asarray(v, jnp.int32) for v in (*ids, *bases, inner, rep_now)]
        count = len(ids)
        wide = max(domains.shape[0], 128)

        def fit(rows):
            return jnp.pad(rows, ((0, 0), (0, wide - rows.shape[1])), constant_values=-1)

        scalars = jnp.concatenate([jnp.stack(values), pno_count])[None, :]
        ints = jnp.concatenate([fit(domains.T), fit(near_pair), fit(scalars)], axis=0)
        return (ints, ints, energies), (0, count, 2 * count, 2 * count + 1, 2 * count + 2)

    def pair_base(o, r):
        return (o * rep_count + r) * pairs

    if occ_count == 8 and rep_count == 4:
        layer, side = occ // 2, occ % 2
        inner = (layer == 1) | (layer == 2)
        near_layer = layer ^ 1
        far_end = jnp.where(layer < 2, 3, 0)
        OWN, OUT, MID, SIDE, MID2, SIDE2, CORE, ROW, BOTH = range(9)
        occ_ids = [
            occ,
            near_layer * 2 + side,
            (3 - layer) * 2 + side,
            layer * 2 + 1 - side,
            far_end * 2 + side,
            near_layer * 2 + 1 - side,
        ]
        ids = [o * pairs + 1 for o in occ_ids] + [nobody] * 3
        bases = [pair_base(o, rep) for o in occ_ids]
        bases += [pair_base(occ, rep ^ k) for k in (1, 2, 3)]
        along = [(a, a ^ 2) for a in range(8)]
        middle = [(a, a ^ 6 if 2 <= a < 6 else a) for a in range(8)]
        across = [(a, a ^ 1) for a in range(8)]
        swap_y = [(r, r ^ 2) for r in range(rep_count)]
        swap_core = [(r, r ^ 1) for r in range(rep_count)]

        straight = [(a ^ 4 if 2 <= a < 6 else a ^ 2, a) for a in range(8)]
        oblique = [(a ^ 3, a) for a in range(8)]
        units, exts = {OWN: own}, {OWN: ext}
        for slot, source, axis, perm in (
            (OUT, OWN, "occ", along),
            (MID, OWN, "occ", middle),
            (SIDE, OWN, "occ", across),
            (ROW, OWN, "rep", swap_y),
            (CORE, OWN, "rep", swap_core),
            (MID2, OUT, "occ", middle),
            (SIDE2, OUT, "occ", across),
            (BOTH, ROW, "rep", swap_core),
        ):
            units[slot] = lax.ppermute(units[source], axis, perm)
            if slot in (MID2, SIDE2):
                source, perm = OWN, straight if slot == MID2 else oblique
            exts[slot] = lax.ppermute(exts[source], axis, perm)
        small, places = small_of(ids, bases, inner, rep)
        dense = {}

        def run(plan, keep=(), **kwargs):
            slots = {slot for block in plan for slot in block}
            result, made = contract(
                {slot: dense[slot] for slot in slots if slot in dense},
                {slot: units[slot] for slot in slots if slot not in dense},
                {slot: exts[slot] for slot in slots},
                small,
                places,
                plan,
                kept=keep,
                **kwargs,
            )
            dense.update(made)
            return result

        first = run(
            (
                (OWN, OWN),
                (CORE, OWN),
                (OUT, OWN),
                (MID, OWN),
                (SIDE, OWN),
                (MID, OUT),
                (SIDE, OUT),
                (ROW, OWN),
                (MID, SIDE),
            ),
            keep=(OWN, OUT, MID, SIDE),
            near_slots={OWN: 0, CORE: 1, ROW: 2},
            silent=((CORE, OWN), (ROW, OWN)),
            inner_only=((MID, OWN), (MID, OUT), (SIDE, OUT), (MID, SIDE)),
        )
        crossing = [(MID, SIDE2), (MID2, SIDE), (MID2, SIDE2), (MID2, OUT)]
        tail = run(
            crossing,
            keep=(MID2, SIDE2),
            addends={OUT: first[OUT], SIDE: first[SIDE]},
            inner_only=crossing,
        )
        returned = [
            lax.ppermute(tail[SIDE], "occ", across),
            lax.ppermute(tail[SIDE2], "occ", oblique),
            lax.ppermute(tail[OUT], "occ", along),
        ]
        close = run(
            ((MID2, OWN), (SIDE2, OWN), (BOTH, OWN)),
            addends={OWN: first[OWN]},
            closing=True,
            near_slots={BOTH: 3},
            silent=((BOTH, OWN),),
            inner_only=((MID2, OWN), (SIDE2, OWN)),
        )
        gain = close[OWN] + sum(returned)
        mask = close["shown"]
    else:
        group_units = lax.all_gather(own, "rep", axis=0)
        group_exts = lax.all_gather(ext, "rep", axis=0)
        line_units = lax.all_gather(own, "occ", axis=0)
        line_exts = lax.all_gather(ext, "occ", axis=0)

        def add_near(total, k):
            r = rep ^ k
            small, places = small_of(
                [nobody, nobody], [pair_base(occ, rep), pair_base(occ, r)], 1, r
            )
            part, _ = contract(
                {},
                {0: own, 1: group_units[r]},
                {0: ext, 1: group_exts[r]},
                small,
                places,
                ((1, 0),),
                near_slots={1: 0},
                silent=((1, 0),),
            )
            return total + part[0], None

        def add_far(total, o):
            small, places = small_of(
                [occ * pairs + 1, o * pairs + 1], [pair_base(occ, rep), pair_base(o, rep)], 1, rep
            )
            part, _ = contract(
                {},
                {0: own, 1: line_units[o]},
                {0: ext, 1: line_exts[o]},
                small,
                places,
                ((1, 0),),
            )
            return total + part[0], None

        gain = pack((denominators[:, :, None] + denominators[:, None, :]) * amps.astype(F32))
        mask = pack(live_both.astype(F32))
        gain, _ = lax.scan(add_near, gain, jnp.arange(rep_count, dtype=jnp.int32))
        gain, _ = lax.scan(add_far, gain, jnp.arange(occ_count, dtype=jnp.int32))
    return unpack(jnp.where(mask > 0, gain, 0.0))


def solution(mesh):
    in_specs = (
        P(("occ", "rep"), None, None, None),
        P(("occ", "rep"), None),
        P(("occ", "rep"), None),
        P(("occ", "rep")),
        P(),
        P(("occ", "rep"), None),
        P(("occ", "rep"), None),
        P(("occ", "rep"), None),
    )
    out_specs = P(("occ", "rep"), None)
    return jax.shard_map(
        residual_of, mesh=mesh, in_specs=in_specs, out_specs=out_specs, check_vma=False
    )
```

time: 353 us -> 80 us (0.23)
  the two profiles are of different devices: /device:TPU:8 before, /device:TPU:0 now
where the time goes in v2:
time: 80 us; the launch traced here: 79.2 us
  starting transfers between devices  31.8 us (40%)
  waiting for transfers between devices  20.1 us (25%)
  Pallas kernels  19.3 us (24%)
  local copies, waits for them, and re-layouts  5.19 us (6%)
  other arithmetic  2.64 us (3%)
    pallas_call x3, Pallas kernels, contract(): pl.pallas_call(body, out_shape=[jax.ShapeDtypeStruct((pairs // 2, NPNO, 1...  19.3 us
    ppermute x8, starting transfers between devices, residual_of(): units[slot] = lax.ppermute(units[source], axis, perm)  15.8 us
    ppermute x8, waiting for transfers between devices, residual_of(): exts[slot] = lax.ppermute(exts[source], axis, perm)  11.7 us
    ppermute x8, starting transfers between devices, residual_of(): exts[slot] = lax.ppermute(exts[source], axis, perm)  11.3 us
    ppermute x8, waiting for transfers between devices, residual_of(): units[slot] = lax.ppermute(units[source], axis, perm)  8.28 us
    ppermute x1, starting transfers between devices, residual_of(): lax.ppermute(tail[SIDE2], 'occ', oblique)  3.15 us
  transfers between devices with their start and end apart: 19, of which 4 were waited for; matrix products, arithmetic and copies ran while one was open for 7% of the time, Pallas kernels for 24%

profile of v2, /device:TPU:0, one launch (start us, length us, event | category | flops | bytes accessed | tf_op | source)
XLA Modules:
  0.0 79.2 jit_solution(16641567961179116218)
XLA Ops:
  0.0 3.0 %collective-permute-start.4 = (bf16[48,64,128]{2,1,0:T(8,128)(2,1)}, bf16[48,64,128]{2,1,0:T(8,128)(2,1)S(1)}, u32[]{:S(2)}, u32[]{:S(2)}) collective-permute-start(bf16[48,64,128]{2,1,0:T(8,128)(2,1)} %bitcast.28), channel_id=1, source_target_pairs={{0,2},{1,3},{2,0},{3,1},{4,6},{5,7},{6,4},{7,5},{8,10},{9,11},{10,... | collective-permute-start | bytes 2359304 | tf_op jit(solution)/shard_map/ppermute | solution.py:304
  3.0 1.6 %collective-permute-start = (bf16[48,64,128]{2,1,0:T(8,128)(2,1)}, bf16[48,64,128]{2,1,0:T(8,128)(2,1)S(1)}, u32[]{:S(2)}, u32[]{:S(2)}) collective-permute-start(bf16[48,64,128]{2,1,0:T(8,128)(2,1)} %bitcast.29), channel_id=1, source_target_pairs={{0,8},{4,12},{8,0},{12,4},{16,24},{20,28},{24,16},{28,20},{1,9},{5... | collective-permute-start | bytes 2359304 | tf_op jit(solution)/shard_map/ppermute | solution.py:304
  4.6 0.7 add_convert_fusion
  5.7 0.7 lt.35
  6.7 0.9 %reshape.68 = bf16[2,2,64,64]{3,2,1,0:T(8,128)(2,1)S(1)} reshape(bf16[4,4096]{1,0:T(4,128)(2,1)} %param.9) | data formatting | bytes 65536 | tf_op jit(solution)/shard_map/reshape | solution.py:234
  8.7 1.5 %collective-permute-start.7 = (bf16[2,72,128]{2,1,0:T(8,128)(2,1)S(1)}, bf16[2,72,128]{2,1,0:T(8,128)(2,1)S(1)}, u32[]{:S(2)}, u32[]{:S(2)}) collective-permute-start(bf16[2,72,128]{2,1,0:T(8,128)(2,1)S(1)} %maximum_maximum_fusion.refs_6_.refs_4_), channel_id=1, source_target_pairs={{0,4},{4,0},{8,12},{12,8},{16,20},{20,16},{24,28},{28,24},{1,5},{5... | collective-permute-start | bytes 110600 | tf_op jit(solution)/shard_map/ppermute | solution.py:307
  10.2 11.4 %collective-permute-done.9.refs_11_ = bf16[2,72,128]{2,1,0:T(8,128)(2,1)S(1)} collective-permute-done((bf16[2,72,128]{2,1,0:T(8,128)(2,1)S(1)}, bf16[2,72,128]{2,1,0:T(8,128)(2,1)S(1)}, u32[]{:S(2)}, u32[]{:S(2)}) %collective-permute-start.9) | collective-permute-done | bytes 36896 | tf_op jit(solution)/shard_map/ppermute | solution.py:307
  22.2 4.7 %collective-permute-start.5 = (bf16[2,72,128]{2,1,0:T(8,128)(2,1)S(1)}, bf16[2,72,128]{2,1,0:T(8,128)(2,1)S(1)}, u32[]{:S(2)}, u32[]{:S(2)}) collective-permute-start(bf16[2,72,128]{2,1,0:T(8,128)(2,1)S(1)} %maximum_maximum_fusion.refs_6_.refs_4_), channel_id=1, source_target_pairs={{0,8},{4,12},{8,0},{12,4},{16,24},{20,28},{24,16},{28,20},{1,9},{5... | collective-permute-start | bytes 110600 | tf_op jit(solution)/shard_map/ppermute | solution.py:307
  26.9 1.6 %collective-permute-start.2 = (bf16[48,64,128]{2,1,0:T(8,128)(2,1)}, bf16[48,64,128]{2,1,0:T(8,128)(2,1)S(1)}, u32[]{:S(2)}, u32[]{:S(2)}) collective-permute-start(bf16[48,64,128]{2,1,0:T(8,128)(2,1)} %bitcast.31), channel_id=1, source_target_pairs={{0,4},{4,0},{8,12},{12,8},{16,20},{20,16},{24,28},{28,24},{1,5},{5... | collective-permute-start | bytes 2359304 | tf_op jit(solution)/shard_map/ppermute | solution.py:304
  28.8 7.4 %collective-permute-start.1 = (bf16[48,64,128]{2,1,0:T(8,128)(2,1)}, bf16[48,64,128]{2,1,0:T(8,128)(2,1)}, u32[]{:S(2)}, u32[]{:S(2)}) collective-permute-start(bf16[48,64,128]{2,1,0:T(8,128)(2,1)} %bitcast.32), channel_id=1, source_target_pairs={{0,0},{4,4},{8,16},{12,20},{16,8},{20,12},{24,24},{28,28},{1,1},{5... | collective-permute-start | bytes 2359304 | tf_op jit(solution)/shard_map/ppermute | solution.py:304
  36.3 0.7 concatenate.12
  37.0 1.6 %collective-permute-start.11 = (bf16[48,64,128]{2,1,0:T(8,128)(2,1)S(1)}, bf16[48,64,128]{2,1,0:T(8,128)(2,1)S(1)}, u32[]{:S(2)}, u32[]{:S(2)}) collective-permute-start(bf16[48,64,128]{2,1,0:T(8,128)(2,1)S(1)} %collective-permute-done.refs_1_), channel_id=1, source_target_pairs={{0,4},{4,0},{8,12},{12,8},{16,20},{20,16},{24,28},{28,24},{1,5},{5... | collective-permute-start | bytes 2359304 | tf_op jit(solution)/shard_map/ppermute | solution.py:304
  39.3 0.8 %pad_maximum_fusion.energies = f32[4,128]{1,0:T(4,128)S(1)} fusion(f32[4,64]{1,0:T(4,128)} %param.10), kind=kLoop, calls=%fused_computation.10 | loop fusion | flops 512 | bytes 3072 | tf_op jit(solution)/shard_map/concatenate | solution.py:251
  40.1 0.7 select_add_fusion.ints.chosen
  40.9 7.5 %collective-permute-done.2.refs_3_ = bf16[48,64,128]{2,1,0:T(8,128)(2,1)S(1)} collective-permute-done((bf16[48,64,128]{2,1,0:T(8,128)(2,1)}, bf16[48,64,128]{2,1,0:T(8,128)(2,1)S(1)}, u32[]{:S(2)}, u32[]{:S(2)}) %collective-permute-start.2) | collective-permute-done | bytes 786464 | tf_op jit(solution)/shard_map/ppermute | solution.py:304
  48.4 3.2 %collective-permute-start.12 = (bf16[2,72,128]{2,1,0:T(8,128)(2,1)S(1)}, bf16[2,72,128]{2,1,0:T(8,128)(2,1)S(1)}, u32[]{:S(2)}, u32[]{:S(2)}) collective-permute-start(bf16[2,72,128]{2,1,0:T(8,128)(2,1)S(1)} %maximum_maximum_fusion.refs_6_.refs_4_), channel_id=1, source_target_pairs={{8,0},{12,4},{24,8},{28,12},{0,16},{4,20},{16,24},{20,28},{9,1},{1... | collective-permute-start | bytes 110600 | tf_op jit(solution)/shard_map/ppermute | solution.py:307
  51.6 1.1 %copy-done = bf16[4,12,64,128]{3,2,1,0:T(8,128)(2,1)S(1)} copy-done((bf16[4,12,64,128]{3,2,1,0:T(8,128)(2,1)S(1)}, bf16[4,12,64,128]{3,2,1,0:T(8,128)(2,1)}, u32[]{:S(2)}) %copy-start) | copy-done | bytes 786456
  52.7 10.6 %shard_map.82 = (f32[2,64,128]{2,1,0:T(8,128)S(1)}, f32[2,64,128]{2,1,0:T(8,128)S(1)}, f32[2,64,128]{2,1,0:T(8,128)S(1)}, bf16[256,4096]{1,0:T(8,128)(2,1)S(1)},...) custom-call(s32[17,128]{1,0:T(8,128)S(1)} %select_add_fusion.ints.chosen, ...), custom_call_target="tpu_custom_call" | custom-call | flops 6341787648 | tf_op jit(solution)/shard_map/pallas_call | solution.py:183
  63.9 0.8 collective-permute-done.11.refs_4_
  64.7 4.5 %shard_map.83 = (f32[2,64,128]{2,1,0:T(8,128)S(1)}, f32[2,64,128]{2,1,0:T(8,128)S(1)}, f32[2,64,128]{2,1,0:T(8,128)S(1)}, bf16[256,4096]{1,0:T(8,128)(2,1)S(1)}, bf16[256,4096]{1,0:T(8,128)(2,1)S(1)}) custom-call(s32[17,128]{1,0:T(8,128)S(1)} %select_add_fusion.ints.chosen, s32[17,128]{1,0:T(8,128)S(1)} %select_add_fusion.ints.chosen, ...), custom_call_target="tpu_custom_call" | custom-call | flops 2818572288 | tf_op jit(solution)/shard_map/pallas_call | solution.py:183
  69.3 1.6 %collective-permute-start.16 = (f32[2,64,128]{2,1,0:T(8,128)S(1)}, f32[2,64,128]{2,1,0:T(8,128)S(1)}, u32[]{:S(2)}, u32[]{:S(2)}) collective-permute-start(f32[2,64,128]{2,1,0:T(8,128)S(1)} %get-tuple-element.30), channel_id=1, source_target_pairs={{0,4},{4,0},{8,12},{12,8},{16,20},{20,16},{24,28},{28,24},{1,5},{5... | collective-permute-start | bytes 196616 | tf_op jit(solution)/shard_map/ppermute | solution.py:351
  70.8 3.2 %collective-permute-start.17 = (f32[2,64,128]{2,1,0:T(8,128)S(1)}, f32[2,64,128]{2,1,0:T(8,128)S(1)}, u32[]{:S(2)}, u32[]{:S(2)}) collective-permute-start(f32[2,64,128]{2,1,0:T(8,128)S(1)} %get-tuple-element.31), channel_id=1, source_target_pairs={{12,0},{8,4},{4,8},{0,12},{28,16},{24,20},{20,24},{16,28},{13,1},{... | collective-permute-start | bytes 196616 | tf_op jit(solution)/shard_map/ppermute | solution.py:352
  74.0 4.2 %shard_map.84 = (f32[2,64,128]{2,1,0:T(8,128)S(1)}, f32[2,64,128]{2,1,0:T(8,128)S(1)}) custom-call(s32[17,128]{1,0:T(8,128)S(1)} %select_add_fusion.ints.chosen, s32[17,128]{1,0:T(8,128)S(1)} %select_add_fusion.ints.chosen, f32[4,128]{1,0:T(4,128)S(1)} %pad_maximum_fusion.energies, bf16[256,4096]{1,0:T(8,128)(2,1)S(1)} %get-tuple-element.19.refs_0_, ...), custom_call_target="tpu_custom_call" | custom-call | flops 2113929216 | tf_op jit(solution)/shard_map/pallas_call | solution.py:183
  78.4 0.7 reshape.73
  (44 shorter events, 4.4 us)
Async XLA Ops:
  0.0 38.6 %collective-permute-start.4 = (bf16[48,64,128]{2,1,0:T(8,128)(2,1)}, bf16[48,64,128]{2,1,0:T(8,128)(2,1)S(1)}, u32[]{:S(2)}, u32[]{:S(2)}) collective-permute-start(bf16[48,64,128]{2,1,0:T(8,128)(2,1)} %bitcast.28), channel_id=1, source_target_pairs={{0,2},{1,3},{2,0},{3,1},{4,6},{5,7},{6,4},{7,5},{8,10},{9,11},{10,... | collective-permute-start | bytes 2359304 | tf_op jit(solution)/shard_map/ppermute | solution.py:304
  3.0 34.0 %collective-permute-start = (bf16[48,64,128]{2,1,0:T(8,128)(2,1)}, bf16[48,64,128]{2,1,0:T(8,128)(2,1)S(1)}, u32[]{:S(2)}, u32[]{:S(2)}) collective-permute-start(bf16[48,64,128]{2,1,0:T(8,128)(2,1)} %bitcast.29), channel_id=1, source_target_pairs={{0,8},{4,12},{8,0},{12,4},{16,24},{20,28},{24,16},{28,20},{1,9},{5... | collective-permute-start | bytes 2359304 | tf_op jit(solution)/shard_map/ppermute | solution.py:304
  8.1 13.4 %collective-permute-start.9 = (bf16[2,72,128]{2,1,0:T(8,128)(2,1)S(1)}, bf16[2,72,128]{2,1,0:T(8,128)(2,1)S(1)}, u32[]{:S(2)}, u32[]{:S(2)}) collective-permute-start(bf16[2,72,128]{2,1,0:T(8,128)(2,1)S(1)} %maximum_maximum_fusion.refs_6_.refs_4_), channel_id=1, source_target_pairs={{0,2},{1,3},{2,0},{3,1},{4,6},{5,7},{6,4},{7,5},{8,10},{9,11},{10,... | collective-permute-start | bytes 110600 | tf_op jit(solution)/shard_map/ppermute | solution.py:307
  8.7 13.5 %collective-permute-start.8 = (bf16[2,72,128]{2,1,0:T(8,128)(2,1)S(1)}, bf16[2,72,128]{2,1,0:T(8,128)(2,1)S(1)}, u32[]{:S(2)}, u32[]{:S(2)}) collective-permute-start(bf16[2,72,128]{2,1,0:T(8,128)(2,1)S(1)} %maximum_maximum_fusion.refs_6_.refs_4_), channel_id=1, source_target_pairs={{0,1},{1,0},{2,3},{3,2},{4,5},{5,4},{6,7},{7,6},{8,9},{9,8},{10,11... | collective-permute-start | bytes 110600 | tf_op jit(solution)/shard_map/ppermute | solution.py:307
  8.7 18.2 %collective-permute-start.7 = (bf16[2,72,128]{2,1,0:T(8,128)(2,1)S(1)}, bf16[2,72,128]{2,1,0:T(8,128)(2,1)S(1)}, u32[]{:S(2)}, u32[]{:S(2)}) collective-permute-start(bf16[2,72,128]{2,1,0:T(8,128)(2,1)S(1)} %maximum_maximum_fusion.refs_6_.refs_4_), channel_id=1, source_target_pairs={{0,4},{4,0},{8,12},{12,8},{16,20},{20,16},{24,28},{28,24},{1,5},{5... | collective-permute-start | bytes 110600 | tf_op jit(solution)/shard_map/ppermute | solution.py:307
  21.5 5.4 %collective-permute-start.6 = (bf16[2,72,128]{2,1,0:T(8,128)(2,1)S(1)}, bf16[2,72,128]{2,1,0:T(8,128)(2,1)S(1)}, u32[]{:S(2)}, u32[]{:S(2)}) collective-permute-start(bf16[2,72,128]{2,1,0:T(8,128)(2,1)S(1)} %maximum_maximum_fusion.refs_6_.refs_4_), channel_id=1, source_target_pairs={{0,0},{4,4},{8,16},{12,20},{16,8},{20,12},{24,24},{28,28},{1,1},{5... | collective-permute-start | bytes 110600 | tf_op jit(solution)/shard_map/ppermute | solution.py:307
  22.2 6.6 %collective-permute-start.5 = (bf16[2,72,128]{2,1,0:T(8,128)(2,1)S(1)}, bf16[2,72,128]{2,1,0:T(8,128)(2,1)S(1)}, u32[]{:S(2)}, u32[]{:S(2)}) collective-permute-start(bf16[2,72,128]{2,1,0:T(8,128)(2,1)S(1)} %maximum_maximum_fusion.refs_6_.refs_4_), channel_id=1, source_target_pairs={{0,8},{4,12},{8,0},{12,4},{16,24},{20,28},{24,16},{28,20},{1,9},{5... | collective-permute-start | bytes 110600 | tf_op jit(solution)/shard_map/ppermute | solution.py:307
  26.9 13.9 %collective-permute-start.3 = (bf16[48,64,128]{2,1,0:T(8,128)(2,1)}, bf16[48,64,128]{2,1,0:T(8,128)(2,1)S(1)}, u32[]{:S(2)}, u32[]{:S(2)}) collective-permute-start(bf16[48,64,128]{2,1,0:T(8,128)(2,1)} %bitcast.30), channel_id=1, source_target_pairs={{0,1},{1,0},{2,3},{3,2},{4,5},{5,4},{6,7},{7,6},{8,9},{9,8},{10,11... | collective-permute-start | bytes 2359304 | tf_op jit(solution)/shard_map/ppermute | solution.py:304
  26.9 21.5 %collective-permute-start.2 = (bf16[48,64,128]{2,1,0:T(8,128)(2,1)}, bf16[48,64,128]{2,1,0:T(8,128)(2,1)S(1)}, u32[]{:S(2)}, u32[]{:S(2)}) collective-permute-start(bf16[48,64,128]{2,1,0:T(8,128)(2,1)} %bitcast.31), channel_id=1, source_target_pairs={{0,4},{4,0},{8,12},{12,8},{16,20},{20,16},{24,28},{28,24},{1,5},{5... | collective-permute-start | bytes 2359304 | tf_op jit(solution)/shard_map/ppermute | solution.py:304
  28.8 22.8 %collective-permute-start.1 = (bf16[48,64,128]{2,1,0:T(8,128)(2,1)}, bf16[48,64,128]{2,1,0:T(8,128)(2,1)}, u32[]{:S(2)}, u32[]{:S(2)}) collective-permute-start(bf16[48,64,128]{2,1,0:T(8,128)(2,1)} %bitcast.32), channel_id=1, source_target_pairs={{0,0},{4,4},{8,16},{12,20},{16,8},{20,12},{24,24},{28,28},{1,1},{5... | collective-permute-start | bytes 2359304 | tf_op jit(solution)/shard_map/ppermute | solution.py:304
  37.0 27.7 %collective-permute-start.11 = (bf16[48,64,128]{2,1,0:T(8,128)(2,1)S(1)}, bf16[48,64,128]{2,1,0:T(8,128)(2,1)S(1)}, u32[]{:S(2)}, u32[]{:S(2)}) collective-permute-start(bf16[48,64,128]{2,1,0:T(8,128)(2,1)S(1)} %collective-permute-done.refs_1_), channel_id=1, source_target_pairs={{0,4},{4,0},{8,12},{12,8},{16,20},{20,16},{24,28},{28,24},{1,5},{5... | collective-permute-start | bytes 2359304 | tf_op jit(solution)/shard_map/ppermute | solution.py:304
  38.6 26.1 %collective-permute-start.10 = (bf16[48,64,128]{2,1,0:T(8,128)(2,1)S(1)}, bf16[48,64,128]{2,1,0:T(8,128)(2,1)S(1)}, u32[]{:S(2)}, u32[]{:S(2)}) collective-permute-start(bf16[48,64,128]{2,1,0:T(8,128)(2,1)S(1)} %collective-permute-done.refs_1_), channel_id=1, source_target_pairs={{0,0},{4,4},{8,16},{12,20},{16,8},{20,12},{24,24},{28,28},{1,1},{5... | collective-permute-start | bytes 2359304 | tf_op jit(solution)/shard_map/ppermute | solution.py:304
  40.8 22.5 %collective-permute-start.13 = (bf16[2,72,128]{2,1,0:T(8,128)(2,1)S(1)}, bf16[2,72,128]{2,1,0:T(8,128)(2,1)S(1)}, u32[]{:S(2)}, u32[]{:S(2)}) collective-permute-start(bf16[2,72,128]{2,1,0:T(8,128)(2,1)S(1)} %maximum_maximum_fusion.refs_6_.refs_4_), channel_id=1, source_target_pairs={{12,0},{8,4},{4,8},{0,12},{28,16},{24,20},{20,24},{16,28},{13,1},{... | collective-permute-start | bytes 110600 | tf_op jit(solution)/shard_map/ppermute | solution.py:307
  48.4 15.5 %collective-permute-start.12 = (bf16[2,72,128]{2,1,0:T(8,128)(2,1)S(1)}, bf16[2,72,128]{2,1,0:T(8,128)(2,1)S(1)}, u32[]{:S(2)}, u32[]{:S(2)}) collective-permute-start(bf16[2,72,128]{2,1,0:T(8,128)(2,1)S(1)} %maximum_maximum_fusion.refs_6_.refs_4_), channel_id=1, source_target_pairs={{8,0},{12,4},{24,8},{28,12},{0,16},{4,20},{16,24},{20,28},{9,1},{1... | collective-permute-start | bytes 110600 | tf_op jit(solution)/shard_map/ppermute | solution.py:307
  51.6 22.4 %collective-permute-start.14 = (bf16[48,64,128]{2,1,0:T(8,128)(2,1)S(1)}, bf16[48,64,128]{2,1,0:T(8,128)(2,1)S(1)}, u32[]{:S(2)}, u32[]{:S(2)}) collective-permute-start(bf16[48,64,128]{2,1,0:T(8,128)(2,1)S(1)} %collective-permute-done.4.refs_5_), channel_id=1, source_target_pairs={{0,1},{1,0},{2,3},{3,2},{4,5},{5,4},{6,7},{7,6},{8,9},{9,8},{10,11... | collective-permute-start | bytes 2359304 | tf_op jit(solution)/shard_map/ppermute | solution.py:304
  51.6 1.1 %copy-start = (bf16[4,12,64,128]{3,2,1,0:T(8,128)(2,1)S(1)}, bf16[4,12,64,128]{3,2,1,0:T(8,128)(2,1)}, u32[]{:S(2)}) copy-start(bf16[4,12,64,128]{3,2,1,0:T(8,128)(2,1)} %param.8) | copy-start | bytes 2359300
  63.3 10.6 %collective-permute-start.15 = (bf16[2,72,128]{2,1,0:T(8,128)(2,1)S(1)}, bf16[2,72,128]{2,1,0:T(8,128)(2,1)S(1)}, u32[]{:S(2)}, u32[]{:S(2)}) collective-permute-start(bf16[2,72,128]{2,1,0:T(8,128)(2,1)S(1)} %collective-permute-done.9.refs_11_), channel_id=1, source_target_pairs={{0,1},{1,0},{2,3},{3,2},{4,5},{5,4},{6,7},{7,6},{8,9},{9,8},{10,11... | collective-permute-start | bytes 110600 | tf_op jit(solution)/shard_map/ppermute | solution.py:307
  69.3 8.9 %collective-permute-start.16 = (f32[2,64,128]{2,1,0:T(8,128)S(1)}, f32[2,64,128]{2,1,0:T(8,128)S(1)}, u32[]{:S(2)}, u32[]{:S(2)}) collective-permute-start(f32[2,64,128]{2,1,0:T(8,128)S(1)} %get-tuple-element.30), channel_id=1, source_target_pairs={{0,4},{4,0},{8,12},{12,8},{16,20},{20,16},{24,28},{28,24},{1,5},{5... | collective-permute-start | bytes 196616 | tf_op jit(solution)/shard_map/ppermute | solution.py:351
  70.8 7.4 %collective-permute-start.17 = (f32[2,64,128]{2,1,0:T(8,128)S(1)}, f32[2,64,128]{2,1,0:T(8,128)S(1)}, u32[]{:S(2)}, u32[]{:S(2)}) collective-permute-start(f32[2,64,128]{2,1,0:T(8,128)S(1)} %get-tuple-element.31), channel_id=1, source_target_pairs={{12,0},{8,4},{4,8},{0,12},{28,16},{24,20},{20,24},{16,28},{13,1},{... | collective-permute-start | bytes 196616 | tf_op jit(solution)/shard_map/ppermute | solution.py:352
  74.0 4.3 %collective-permute-start.18 = (f32[2,64,128]{2,1,0:T(8,128)S(1)}, f32[2,64,128]{2,1,0:T(8,128)S(1)}, u32[]{:S(2)}, u32[]{:S(2)}) collective-permute-start(f32[2,64,128]{2,1,0:T(8,128)S(1)} %get-tuple-element.32), channel_id=1, source_target_pairs={{0,8},{4,12},{8,0},{12,4},{16,24},{20,28},{24,16},{28,20},{1,9},{5... | collective-permute-start | bytes 196616 | tf_op jit(solution)/shard_map/ppermute | solution.py:353

commit v3 on v2

--- a/solution.py
+++ b/solution.py
@@ -340,6 +340,10 @@
             silent=((CORE, OWN), (ROW, OWN)),
             inner_only=((MID, OWN), (MID, OUT), (SIDE, OUT), (MID, SIDE)),
         )
+        apart = run(
+            ((BOTH, OWN),), addends={OWN: first[OWN]}, near_slots={BOTH: 3}, silent=((BOTH, OWN),)
+        )
+        first[OUT], apart[OWN] = lax.optimization_barrier((first[OUT], apart[OWN]))
         crossing = [(MID, SIDE2), (MID2, SIDE), (MID2, SIDE2), (MID2, OUT)]
         tail = run(
             crossing,
@@ -353,11 +357,9 @@
             lax.ppermute(tail[OUT], "occ", along),
         ]
         close = run(
-            ((MID2, OWN), (SIDE2, OWN), (BOTH, OWN)),
-            addends={OWN: first[OWN]},
+            ((MID2, OWN), (SIDE2, OWN)),
+            addends={OWN: apart[OWN]},
             closing=True,
-            near_slots={BOTH: 3},
-            silent=((BOTH, OWN),),
             inner_only=((MID2, OWN), (SIDE2, OWN)),
         )
         gain = close[OWN] + sum(returned)

time: 80 us -> 83.7 us (1.046)
  waiting for transfers between devices: 20.1 us -> 27.4 us
  starting transfers between devices: 31.8 us -> 26.5 us
  Pallas kernels: 19.3 us -> 21.4 us
    ppermute x8, waiting for transfers between devices: 8.28 us -> 14.6 us  [residual_of(): units[slot] = lax.ppermute(units[source], axis, perm)]
    ppermute x8, starting transfers between devices: 15.8 us -> 10.1 us  [residual_of(): units[slot] = lax.ppermute(units[source], axis, perm)]
    ppermute x1, starting transfers between devices: 3.15 us -> 0.57 us  [residual_of(): lax.ppermute(tail[SIDE2], 'occ', oblique)]
    pallas_call x3 -> x4, Pallas kernels: 19.3 us -> 21.4 us  [contract(): pl.pallas_call(body, out_shape=[jax.ShapeDtypeStruct((pairs // 2, NPNO, 1...]
    ppermute x8, starting transfers between devices: 11.3 us -> 12.8 us  [residual_of(): exts[slot] = lax.ppermute(exts[source], axis, perm)]
    ppermute x1, starting transfers between devices: 0.01 us -> 1.41 us  [residual_of(): lax.ppermute(tail[OUT], 'occ', along)]
  transfers between devices with their start and end apart: 19 -> 19, of which waited for: 4 -> 6; matrix products, arithmetic and copies ran while one was open for 7% -> 7% of each run, Pallas kernels for 24% -> 19%
where the time goes in v3:
time: 83.7 us; the launch traced here: 83.2 us
  waiting for transfers between devices  27.4 us (33%)
  starting transfers between devices  26.5 us (32%)
  Pallas kernels  21.4 us (26%)
  local copies, waits for them, and re-layouts  5.18 us (6%)
  other arithmetic  2.65 us (3%)
    pallas_call x4, Pallas kernels, contract(): pl.pallas_call(body, out_shape=[jax.ShapeDtypeStruct((pairs // 2, NPNO, 1...  21.4 us
    ppermute x8, waiting for transfers between devices, residual_of(): units[slot] = lax.ppermute(units[source], axis, perm)  14.6 us
    ppermute x8, starting transfers between devices, residual_of(): exts[slot] = lax.ppermute(exts[source], axis, perm)  12.8 us
    ppermute x8, waiting for transfers between devices, residual_of(): exts[slot] = lax.ppermute(exts[source], axis, perm)  12.5 us
    ppermute x8, starting transfers between devices, residual_of(): units[slot] = lax.ppermute(units[source], axis, perm)  10.1 us
  transfers between devices with their start and end apart: 19, of which 6 were waited for; matrix products, arithmetic and copies ran while one was open for 7% of the time, Pallas kernels for 19%

profile of v3, /device:TPU:0, one launch (start us, length us, event | category | flops | bytes accessed | tf_op | source)
XLA Modules:
  0.0 83.2 jit_solution(1382023174850474805)
XLA Ops:
  0.0 3.1 %collective-permute-start = (bf16[48,64,128]{2,1,0:T(8,128)(2,1)}, bf16[48,64,128]{2,1,0:T(8,128)(2,1)S(1)}, u32[]{:S(2)}, u32[]{:S(2)}) collective-permute-start(bf16[48,64,128]{2,1,0:T(8,128)(2,1)} %bitcast.28), channel_id=1, source_target_pairs={{0,8},{4,12},{8,0},{12,4},{16,24},{20,28},{24,16},{28,20},{1,9},{5... | collective-permute-start | bytes 2359304 | tf_op jit(solution)/shard_map/ppermute | solution.py:304
  3.1 1.5 %collective-permute-start.4 = (bf16[48,64,128]{2,1,0:T(8,128)(2,1)}, bf16[48,64,128]{2,1,0:T(8,128)(2,1)S(1)}, u32[]{:S(2)}, u32[]{:S(2)}) collective-permute-start(bf16[48,64,128]{2,1,0:T(8,128)(2,1)} %bitcast.29), channel_id=1, source_target_pairs={{0,2},{1,3},{2,0},{3,1},{4,6},{5,7},{6,4},{7,5},{8,10},{9,11},{10,... | collective-permute-start | bytes 2359304 | tf_op jit(solution)/shard_map/ppermute | solution.py:304
  4.6 1.8 %collective-permute-start.1 = (bf16[48,64,128]{2,1,0:T(8,128)(2,1)}, bf16[48,64,128]{2,1,0:T(8,128)(2,1)S(1)}, u32[]{:S(2)}, u32[]{:S(2)}) collective-permute-start(bf16[48,64,128]{2,1,0:T(8,128)(2,1)} %bitcast.30), channel_id=1, source_target_pairs={{0,0},{4,4},{8,16},{12,20},{16,8},{20,12},{24,24},{28,28},{1,1},{5... | collective-permute-start | bytes 2359304 | tf_op jit(solution)/shard_map/ppermute | solution.py:304
  8.2 0.9 %reshape.68 = bf16[2,2,64,64]{3,2,1,0:T(8,128)(2,1)S(1)} reshape(bf16[4,4096]{1,0:T(4,128)(2,1)} %param.9) | data formatting | bytes 65536 | tf_op jit(solution)/shard_map/reshape | solution.py:234
  9.9 3.3 %collective-permute-start.5 = (bf16[2,72,128]{2,1,0:T(8,128)(2,1)S(1)}, bf16[2,72,128]{2,1,0:T(8,128)(2,1)S(1)}, u32[]{:S(2)}, u32[]{:S(2)}) collective-permute-start(bf16[2,72,128]{2,1,0:T(8,128)(2,1)S(1)} %maximum_maximum_fusion.refs_6_.refs_2_.refs_3_), channel_id=1, source_target_pairs={{0,8},{4,12},{8,0},{12,4},{16,24},{20,28},{24,16},{28,20},{1,9},{5... | collective-permute-start | bytes 110600 | tf_op jit(solution)/shard_map/ppermute | solution.py:307
  13.9 7.7 %collective-permute-done.5.refs_7_.refs_5_ = bf16[2,72,128]{2,1,0:T(8,128)(2,1)S(1)} collective-permute-done((bf16[2,72,128]{2,1,0:T(8,128)(2,1)S(1)}, bf16[2,72,128]{2,1,0:T(8,128)(2,1)S(1)}, u32[]{:S(2)}, u32[]{:S(2)}) %collective-permute-start.5) | collective-permute-done | bytes 36896 | tf_op jit(solution)/shard_map/ppermute | solution.py:307
  21.6 1.7 %collective-permute-start.7 = (bf16[2,72,128]{2,1,0:T(8,128)(2,1)S(1)}, bf16[2,72,128]{2,1,0:T(8,128)(2,1)S(1)}, u32[]{:S(2)}, u32[]{:S(2)}) collective-permute-start(bf16[2,72,128]{2,1,0:T(8,128)(2,1)S(1)} %maximum_maximum_fusion.refs_6_.refs_2_.refs_3_), channel_id=1, source_target_pairs={{0,4},{4,0},{8,12},{12,8},{16,20},{20,16},{24,28},{28,24},{1,5},{5... | collective-permute-start | bytes 110600 | tf_op jit(solution)/shard_map/ppermute | solution.py:307
  23.3 1.5 %collective-permute-start.9 = (bf16[2,72,128]{2,1,0:T(8,128)(2,1)S(1)}, bf16[2,72,128]{2,1,0:T(8,128)(2,1)S(1)}, u32[]{:S(2)}, u32[]{:S(2)}) collective-permute-start(bf16[2,72,128]{2,1,0:T(8,128)(2,1)S(1)} %maximum_maximum_fusion.refs_6_.refs_2_.refs_3_), channel_id=1, source_target_pairs={{0,2},{1,3},{2,0},{3,1},{4,6},{5,7},{6,4},{7,5},{8,10},{9,11},{10,... | collective-permute-start | bytes 110600 | tf_op jit(solution)/shard_map/ppermute | solution.py:307
  24.8 0.8 collective-permute-done.7.refs_9_.refs_7_
  25.6 1.7 %collective-permute-done.9.refs_11_ = bf16[2,72,128]{2,1,0:T(8,128)(2,1)S(1)} collective-permute-done((bf16[2,72,128]{2,1,0:T(8,128)(2,1)S(1)}, bf16[2,72,128]{2,1,0:T(8,128)(2,1)S(1)}, u32[]{:S(2)}, u32[]{:S(2)}) %collective-permute-start.9) | collective-permute-done | bytes 36896 | tf_op jit(solution)/shard_map/ppermute | solution.py:307
  27.6 1.5 %collective-permute-start.10 = (bf16[48,64,128]{2,1,0:T(8,128)(2,1)S(1)}, bf16[48,64,128]{2,1,0:T(8,128)(2,1)}, u32[]{:S(2)}, u32[]{:S(2)}) collective-permute-start(bf16[48,64,128]{2,1,0:T(8,128)(2,1)S(1)} %collective-permute-done.refs_1_), channel_id=1, source_target_pairs={{0,0},{4,4},{8,16},{12,20},{16,8},{20,12},{24,24},{28,28},{1,1},{5... | collective-permute-start | bytes 2359304 | tf_op jit(solution)/shard_map/ppermute | solution.py:304
  29.1 1.7 %collective-permute-start.11 = (bf16[48,64,128]{2,1,0:T(8,128)(2,1)S(1)}, bf16[48,64,128]{2,1,0:T(8,128)(2,1)}, u32[]{:S(2)}, u32[]{:S(2)}) collective-permute-start(bf16[48,64,128]{2,1,0:T(8,128)(2,1)S(1)} %collective-permute-done.refs_1_), channel_id=1, source_target_pairs={{0,4},{4,0},{8,12},{12,8},{16,20},{20,16},{24,28},{28,24},{1,5},{5... | collective-permute-start | bytes 2359304 | tf_op jit(solution)/shard_map/ppermute | solution.py:304
  31.0 0.8 pad_maximum_fusion.energies
  31.9 0.7 concatenate.12
  33.3 14.6 %collective-permute-done.2.refs_3_ = bf16[48,64,128]{2,1,0:T(8,128)(2,1)} collective-permute-done((bf16[48,64,128]{2,1,0:T(8,128)(2,1)}, bf16[48,64,128]{2,1,0:T(8,128)(2,1)}, u32[]{:S(2)}, u32[]{:S(2)}) %collective-permute-start.2) | collective-permute-done | bytes 786464 | tf_op jit(solution)/shard_map/ppermute | solution.py:304
  47.9 5.5 %collective-permute-start.12 = (bf16[2,72,128]{2,1,0:T(8,128)(2,1)S(1)}, bf16[2,72,128]{2,1,0:T(8,128)(2,1)S(1)}, u32[]{:S(2)}, u32[]{:S(2)}) collective-permute-start(bf16[2,72,128]{2,1,0:T(8,128)(2,1)S(1)} %maximum_maximum_fusion.refs_6_.refs_2_.refs_3_), channel_id=1, source_target_pairs={{8,0},{12,4},{24,8},{28,12},{0,16},{4,20},{16,24},{20,28},{9,1},{1... | collective-permute-start | bytes 110600 | tf_op jit(solution)/shard_map/ppermute | solution.py:307
  53.5 1.1 %copy-done = bf16[4,12,64,128]{3,2,1,0:T(8,128)(2,1)S(1)} copy-done((bf16[4,12,64,128]{3,2,1,0:T(8,128)(2,1)S(1)}, bf16[4,12,64,128]{3,2,1,0:T(8,128)(2,1)}, u32[]{:S(2)}) %copy-start) | copy-done | bytes 786456
  54.6 10.6 %shard_map.82 = (f32[2,64,128]{2,1,0:T(8,128)S(1)}, f32[2,64,128]{2,1,0:T(8,128)S(1)}, f32[2,64,128]{2,1,0:T(8,128)S(1)}, bf16[256,4096]{1,0:T(8,128)(2,1)S(1)},...) custom-call(s32[17,128]{1,0:T(8,128)S(1)} %select_add_fusion.ints.chosen, ...), custom_call_target="tpu_custom_call" | custom-call | flops 6341787648 | tf_op jit(solution)/shard_map/pallas_call | solution.py:183
  65.3 2.4 %shard_map.83.refs_6_ = f32[2,64,128]{2,1,0:T(8,128)S(1)} custom-call(s32[17,128]{1,0:T(8,128)S(1)} %select_add_fusion.ints.chosen, s32[17,128]{1,0:T(8,128)S(1)} %select_add_fusion.ints.chosen, f32[4,128]{1,0:T(4,128)S(1)} %pad_maximum_fusion.energies, bf16[256,4096]{1,0:T(8,128)(2,1)S(1)} %get-tuple-element.21.refs_0_, ...), custom_call_target="tpu_custom_call" | custom-call | flops 704643072 | tf_op jit(solution)/shard_map/pallas_call | solution.py:183
  67.7 2.4 %collective-permute-done.13.refs_9_.refs_5_ = bf16[2,72,128]{2,1,0:T(8,128)(2,1)S(1)} collective-permute-done((bf16[2,72,128]{2,1,0:T(8,128)(2,1)S(1)}, bf16[2,72,128]{2,1,0:T(8,128)(2,1)S(1)}, u32[]{:S(2)}, u32[]{:S(2)}) %collective-permute-start.13) | collective-permute-done | bytes 36896 | tf_op jit(solution)/shard_map/ppermute | solution.py:307
  70.1 5.4 %shard_map.84 = (f32[2,64,128]{2,1,0:T(8,128)S(1)}, f32[2,64,128]{2,1,0:T(8,128)S(1)}, f32[2,64,128]{2,1,0:T(8,128)S(1)}, bf16[256,4096]{1,0:T(8,128)(2,1)S(1)}, bf16[256,4096]{1,0:T(8,128)(2,1)S(1)}) custom-call(s32[17,128]{1,0:T(8,128)S(1)} %select_add_fusion.ints.chosen, s32[17,128]{1,0:T(8,128)S(1)} %select_add_fusion.ints.chosen, ...), custom_call_target="tpu_custom_call" | custom-call | flops 2818572288 | tf_op jit(solution)/shard_map/pallas_call | solution.py:183
  75.6 1.6 %collective-permute-start.16 = (f32[2,64,128]{2,1,0:T(8,128)S(1)}, f32[2,64,128]{2,1,0:T(8,128)S(1)}, u32[]{:S(2)}, u32[]{:S(2)}) collective-permute-start(f32[2,64,128]{2,1,0:T(8,128)S(1)} %get-tuple-element.34), channel_id=1, source_target_pairs={{0,4},{4,0},{8,12},{12,8},{16,20},{20,16},{24,28},{28,24},{1,5},{5... | collective-permute-start | bytes 196616 | tf_op jit(solution)/shard_map/ppermute | solution.py:355
  77.7 1.4 %collective-permute-start.18 = (f32[2,64,128]{2,1,0:T(8,128)S(1)}, f32[2,64,128]{2,1,0:T(8,128)S(1)}, u32[]{:S(2)}, u32[]{:S(2)}) collective-permute-start(f32[2,64,128]{2,1,0:T(8,128)S(1)} %get-tuple-element.36), channel_id=1, source_target_pairs={{0,8},{4,12},{8,0},{12,4},{16,24},{20,28},{24,16},{28,20},{1,9},{5... | collective-permute-start | bytes 196616 | tf_op jit(solution)/shard_map/ppermute | solution.py:357
  79.1 2.9 %shard_map.85 = (f32[2,64,128]{2,1,0:T(8,128)S(1)}, f32[2,64,128]{2,1,0:T(8,128)S(1)}) custom-call(s32[17,128]{1,0:T(8,128)S(1)} %select_add_fusion.ints.chosen, s32[17,128]{1,0:T(8,128)S(1)} %select_add_fusion.ints.chosen, f32[4,128]{1,0:T(4,128)S(1)} %pad_maximum_fusion.energies, bf16[256,4096]{1,0:T(8,128)(2,1)S(1)} %get-tuple-element.21.refs_0_, ...), custom_call_target="tpu_custom_call" | custom-call | flops 1409286144 | tf_op jit(solution)/shard_map/pallas_call | solution.py:183
  (45 shorter events, 6.4 us)
Async XLA Ops:
  0.0 27.6 %collective-permute-start = (bf16[48,64,128]{2,1,0:T(8,128)(2,1)}, bf16[48,64,128]{2,1,0:T(8,128)(2,1)S(1)}, u32[]{:S(2)}, u32[]{:S(2)}) collective-permute-start(bf16[48,64,128]{2,1,0:T(8,128)(2,1)} %bitcast.28), channel_id=1, source_target_pairs={{0,8},{4,12},{8,0},{12,4},{16,24},{20,28},{24,16},{28,20},{1,9},{5... | collective-permute-start | bytes 2359304 | tf_op jit(solution)/shard_map/ppermute | solution.py:304
  3.1 26.1 %collective-permute-start.4 = (bf16[48,64,128]{2,1,0:T(8,128)(2,1)}, bf16[48,64,128]{2,1,0:T(8,128)(2,1)S(1)}, u32[]{:S(2)}, u32[]{:S(2)}) collective-permute-start(bf16[48,64,128]{2,1,0:T(8,128)(2,1)} %bitcast.29), channel_id=1, source_target_pairs={{0,2},{1,3},{2,0},{3,1},{4,6},{5,7},{6,4},{7,5},{8,10},{9,11},{10,... | collective-permute-start | bytes 2359304 | tf_op jit(solution)/shard_map/ppermute | solution.py:304
  4.6 26.2 %collective-permute-start.1 = (bf16[48,64,128]{2,1,0:T(8,128)(2,1)}, bf16[48,64,128]{2,1,0:T(8,128)(2,1)S(1)}, u32[]{:S(2)}, u32[]{:S(2)}) collective-permute-start(bf16[48,64,128]{2,1,0:T(8,128)(2,1)} %bitcast.30), channel_id=1, source_target_pairs={{0,0},{4,4},{8,16},{12,20},{16,8},{20,12},{24,24},{28,28},{1,1},{5... | collective-permute-start | bytes 2359304 | tf_op jit(solution)/shard_map/ppermute | solution.py:304
  9.9 11.7 %collective-permute-start.5 = (bf16[2,72,128]{2,1,0:T(8,128)(2,1)S(1)}, bf16[2,72,128]{2,1,0:T(8,128)(2,1)S(1)}, u32[]{:S(2)}, u32[]{:S(2)}) collective-permute-start(bf16[2,72,128]{2,1,0:T(8,128)(2,1)S(1)} %maximum_maximum_fusion.refs_6_.refs_2_.refs_3_), channel_id=1, source_target_pairs={{0,8},{4,12},{8,0},{12,4},{16,24},{20,28},{24,16},{28,20},{1,9},{5... | collective-permute-start | bytes 110600 | tf_op jit(solution)/shard_map/ppermute | solution.py:307
  13.2 10.0 %collective-permute-start.6 = (bf16[2,72,128]{2,1,0:T(8,128)(2,1)S(1)}, bf16[2,72,128]{2,1,0:T(8,128)(2,1)S(1)}, u32[]{:S(2)}, u32[]{:S(2)}) collective-permute-start(bf16[2,72,128]{2,1,0:T(8,128)(2,1)S(1)} %maximum_maximum_fusion.refs_6_.refs_2_.refs_3_), channel_id=1, source_target_pairs={{0,0},{4,4},{8,16},{12,20},{16,8},{20,12},{24,24},{28,28},{1,1},{5... | collective-permute-start | bytes 110600 | tf_op jit(solution)/shard_map/ppermute | solution.py:307
  21.6 4.0 %collective-permute-start.7 = (bf16[2,72,128]{2,1,0:T(8,128)(2,1)S(1)}, bf16[2,72,128]{2,1,0:T(8,128)(2,1)S(1)}, u32[]{:S(2)}, u32[]{:S(2)}) collective-permute-start(bf16[2,72,128]{2,1,0:T(8,128)(2,1)S(1)} %maximum_maximum_fusion.refs_6_.refs_2_.refs_3_), channel_id=1, source_target_pairs={{0,4},{4,0},{8,12},{12,8},{16,20},{20,16},{24,28},{28,24},{1,5},{5... | collective-permute-start | bytes 110600 | tf_op jit(solution)/shard_map/ppermute | solution.py:307
  23.3 4.0 %collective-permute-start.9 = (bf16[2,72,128]{2,1,0:T(8,128)(2,1)S(1)}, bf16[2,72,128]{2,1,0:T(8,128)(2,1)S(1)}, u32[]{:S(2)}, u32[]{:S(2)}) collective-permute-start(bf16[2,72,128]{2,1,0:T(8,128)(2,1)S(1)} %maximum_maximum_fusion.refs_6_.refs_2_.refs_3_), channel_id=1, source_target_pairs={{0,2},{1,3},{2,0},{3,1},{4,6},{5,7},{6,4},{7,5},{8,10},{9,11},{10,... | collective-permute-start | bytes 110600 | tf_op jit(solution)/shard_map/ppermute | solution.py:307
  25.6 2.0 %collective-permute-start.8 = (bf16[2,72,128]{2,1,0:T(8,128)(2,1)S(1)}, bf16[2,72,128]{2,1,0:T(8,128)(2,1)S(1)}, u32[]{:S(2)}, u32[]{:S(2)}) collective-permute-start(bf16[2,72,128]{2,1,0:T(8,128)(2,1)S(1)} %maximum_maximum_fusion.refs_6_.refs_2_.refs_3_), channel_id=1, source_target_pairs={{0,1},{1,0},{2,3},{3,2},{4,5},{5,4},{6,7},{7,6},{8,9},{9,8},{10,11... | collective-permute-start | bytes 110600 | tf_op jit(solution)/shard_map/ppermute | solution.py:307
  27.2 20.7 %collective-permute-start.2 = (bf16[48,64,128]{2,1,0:T(8,128)(2,1)}, bf16[48,64,128]{2,1,0:T(8,128)(2,1)}, u32[]{:S(2)}, u32[]{:S(2)}) collective-permute-start(bf16[48,64,128]{2,1,0:T(8,128)(2,1)} %bitcast.31), channel_id=1, source_target_pairs={{0,4},{4,0},{8,12},{12,8},{16,20},{20,16},{24,28},{28,24},{1,5},{5... | collective-permute-start | bytes 2359304 | tf_op jit(solution)/shard_map/ppermute | solution.py:304
  27.6 25.9 %collective-permute-start.3 = (bf16[48,64,128]{2,1,0:T(8,128)(2,1)}, bf16[48,64,128]{2,1,0:T(8,128)(2,1)}, u32[]{:S(2)}, u32[]{:S(2)}) collective-permute-start(bf16[48,64,128]{2,1,0:T(8,128)(2,1)} %bitcast.32), channel_id=1, source_target_pairs={{0,1},{1,0},{2,3},{3,2},{4,5},{5,4},{6,7},{7,6},{8,9},{9,8},{10,11... | collective-permute-start | bytes 2359304 | tf_op jit(solution)/shard_map/ppermute | solution.py:304
  27.6 42.5 %collective-permute-start.10 = (bf16[48,64,128]{2,1,0:T(8,128)(2,1)S(1)}, bf16[48,64,128]{2,1,0:T(8,128)(2,1)}, u32[]{:S(2)}, u32[]{:S(2)}) collective-permute-start(bf16[48,64,128]{2,1,0:T(8,128)(2,1)S(1)} %collective-permute-done.refs_1_), channel_id=1, source_target_pairs={{0,0},{4,4},{8,16},{12,20},{16,8},{20,12},{24,24},{28,28},{1,1},{5... | collective-permute-start | bytes 2359304 | tf_op jit(solution)/shard_map/ppermute | solution.py:304
  29.1 41.0 %collective-permute-start.11 = (bf16[48,64,128]{2,1,0:T(8,128)(2,1)S(1)}, bf16[48,64,128]{2,1,0:T(8,128)(2,1)}, u32[]{:S(2)}, u32[]{:S(2)}) collective-permute-start(bf16[48,64,128]{2,1,0:T(8,128)(2,1)S(1)} %collective-permute-done.refs_1_), channel_id=1, source_target_pairs={{0,4},{4,0},{8,12},{12,8},{16,20},{20,16},{24,28},{28,24},{1,5},{5... | collective-permute-start | bytes 2359304 | tf_op jit(solution)/shard_map/ppermute | solution.py:304
  30.8 34.5 %collective-permute-start.14 = (bf16[48,64,128]{2,1,0:T(8,128)(2,1)S(1)}, bf16[48,64,128]{2,1,0:T(8,128)(2,1)S(1)}, u32[]{:S(2)}, u32[]{:S(2)}) collective-permute-start(bf16[48,64,128]{2,1,0:T(8,128)(2,1)S(1)} %collective-permute-done.4.refs_5_), channel_id=1, source_target_pairs={{0,1},{1,0},{2,3},{3,2},{4,5},{5,4},{6,7},{7,6},{8,9},{9,8},{10,11... | collective-permute-start | bytes 2359304 | tf_op jit(solution)/shard_map/ppermute | solution.py:304
  47.9 19.8 %collective-permute-start.12 = (bf16[2,72,128]{2,1,0:T(8,128)(2,1)S(1)}, bf16[2,72,128]{2,1,0:T(8,128)(2,1)S(1)}, u32[]{:S(2)}, u32[]{:S(2)}) collective-permute-start(bf16[2,72,128]{2,1,0:T(8,128)(2,1)S(1)} %maximum_maximum_fusion.refs_6_.refs_2_.refs_3_), channel_id=1, source_target_pairs={{8,0},{12,4},{24,8},{28,12},{0,16},{4,20},{16,24},{20,28},{9,1},{1... | collective-permute-start | bytes 110600 | tf_op jit(solution)/shard_map/ppermute | solution.py:307
  53.5 11.7 %collective-permute-start.15 = (bf16[2,72,128]{2,1,0:T(8,128)(2,1)S(1)}, bf16[2,72,128]{2,1,0:T(8,128)(2,1)S(1)}, u32[]{:S(2)}, u32[]{:S(2)}) collective-permute-start(bf16[2,72,128]{2,1,0:T(8,128)(2,1)S(1)} %collective-permute-done.9.refs_11_), channel_id=1, source_target_pairs={{0,1},{1,0},{2,3},{3,2},{4,5},{5,4},{6,7},{7,6},{8,9},{9,8},{10,11... | collective-permute-start | bytes 110600 | tf_op jit(solution)/shard_map/ppermute | solution.py:307
  53.5 1.1 %copy-start = (bf16[4,12,64,128]{3,2,1,0:T(8,128)(2,1)S(1)}, bf16[4,12,64,128]{3,2,1,0:T(8,128)(2,1)}, u32[]{:S(2)}) copy-start(bf16[4,12,64,128]{3,2,1,0:T(8,128)(2,1)} %param.8) | copy-start | bytes 2359300
  65.2 4.9 %collective-permute-start.13 = (bf16[2,72,128]{2,1,0:T(8,128)(2,1)S(1)}, bf16[2,72,128]{2,1,0:T(8,128)(2,1)S(1)}, u32[]{:S(2)}, u32[]{:S(2)}) collective-permute-start(bf16[2,72,128]{2,1,0:T(8,128)(2,1)S(1)} %maximum_maximum_fusion.refs_6_.refs_2_.refs_3_), channel_id=1, source_target_pairs={{12,0},{8,4},{4,8},{0,12},{28,16},{24,20},{20,24},{16,28},{13,1},{... | collective-permute-start | bytes 110600 | tf_op jit(solution)/shard_map/ppermute | solution.py:307
  75.6 6.5 %collective-permute-start.16 = (f32[2,64,128]{2,1,0:T(8,128)S(1)}, f32[2,64,128]{2,1,0:T(8,128)S(1)}, u32[]{:S(2)}, u32[]{:S(2)}) collective-permute-start(f32[2,64,128]{2,1,0:T(8,128)S(1)} %get-tuple-element.34), channel_id=1, source_target_pairs={{0,4},{4,0},{8,12},{12,8},{16,20},{20,16},{24,28},{28,24},{1,5},{5... | collective-permute-start | bytes 196616 | tf_op jit(solution)/shard_map/ppermute | solution.py:355
  77.1 5.2 %collective-permute-start.17 = (f32[2,64,128]{2,1,0:T(8,128)S(1)}, f32[2,64,128]{2,1,0:T(8,128)S(1)}, u32[]{:S(2)}, u32[]{:S(2)}) collective-permute-start(f32[2,64,128]{2,1,0:T(8,128)S(1)} %get-tuple-element.35), channel_id=1, source_target_pairs={{12,0},{8,4},{4,8},{0,12},{28,16},{24,20},{20,24},{16,28},{13,1},{... | collective-permute-start | bytes 196616 | tf_op jit(solution)/shard_map/ppermute | solution.py:356
  77.7 4.6 %collective-permute-start.18 = (f32[2,64,128]{2,1,0:T(8,128)S(1)}, f32[2,64,128]{2,1,0:T(8,128)S(1)}, u32[]{:S(2)}, u32[]{:S(2)}) collective-permute-start(f32[2,64,128]{2,1,0:T(8,128)S(1)} %get-tuple-element.36), channel_id=1, source_target_pairs={{0,8},{4,12},{8,0},{12,4},{16,24},{20,28},{24,16},{28,20},{1,9},{5... | collective-permute-start | bytes 196616 | tf_op jit(solution)/shard_map/ppermute | solution.py:357
